TPU v7x, 32 devices: a 4x4x1 block of a 4x4x8 slice. The times are simulated.
32 devices in a mesh: batch: 1 (over z), sy: 4 (over y), sx: 8 (over x, core).
Axes of the slice: x: 4, y: 4, z: 1, core: 2. Of those that a mesh axis runs over, the one named last changes fastest.
The devices are a block of a 4x4x8 slice.
Arguments:
- forcing: float32 [256, 128, 192], P(('batch', 'sx'), 'sy')
- kappa: float32 [256, 128], P(('batch', 'sx'), 'sy')
- local_inv: float32 [32, 1600, 1600], P(('batch', 'sx', 'sy'))
- coarse_basis: float32 [32, 1024, 8], P(('batch', 'sx', 'sy'))
- coarse_counts: int32 [32], P(('batch', 'sx', 'sy'))
- coarse_inv: float32 [128, 128], P('batch')
Outputs:
- output 1: float32 [256, 128, 192], P(('batch', 'sx'), 'sy')
- output 2: float32 [8, 192], P('batch')
All inputs are finite; a program needn't handle non-finite values.
Results may differ from a plain program's by a relative error of at most 0.001.
Values are sent between devices in bfloat16 or wider.
A program may use at most 768 MiB of HBM per device.

v0:
```python
import math
import jax
import jax.numpy as jnp
from jax import lax
from jax.sharding import PartitionSpec as P

ITERS = 8


def harmonic(first, second):
    return 2.0 * first * second / (first + second)


def solution(mesh):
    n_row = mesh.shape['sx']
    n_col = mesh.shape['sy']
    to_below = [(index, index + 1) for index in range(n_row - 1)]
    to_above = [(index + 1, index) for index in range(n_row - 1)]
    to_right = [(index, index + 1) for index in range(n_col - 1)]
    to_left = [(index + 1, index) for index in range(n_col - 1)]
    grid_axes = ('sx', 'sy')
    highest = lax.Precision.HIGHEST

    def matmul(first, second):
        return jnp.dot(first, second, precision=highest, preferred_element_type=jnp.float32)

    def body(forcing, kappa, local_inv, coarse_basis, coarse_counts, coarse_inv):
        row_id = lax.axis_index('sx')
        col_id = lax.axis_index('sy')
        size = forcing.shape[0]
        n_rhs = forcing.shape[2]
        edge = math.isqrt(local_inv.shape[1])
        over = (edge - size) // 2
        kmax = coarse_basis.shape[2]
        ktot = coarse_inv.shape[0]
        inverse = local_inv[0]
        basis = coarse_basis[0]

        above = lax.ppermute(kappa[-1:], 'sx', to_below)
        below = lax.ppermute(kappa[:1], 'sx', to_above)
        leftside = lax.ppermute(kappa[:, -1:], 'sy', to_right)
        rightside = lax.ppermute(kappa[:, :1], 'sy', to_left)
        above = jnp.where(row_id == 0, kappa[:1], above)
        below = jnp.where(row_id == n_row - 1, kappa[-1:], below)
        leftside = jnp.where(col_id == 0, kappa[:, :1], leftside)
        rightside = jnp.where(col_id == n_col - 1, kappa[:, -1:], rightside)
        w_north = harmonic(kappa, jnp.concatenate([above, kappa[:-1]], axis=0))[:, :, None]
        w_south = harmonic(kappa, jnp.concatenate([kappa[1:], below], axis=0))[:, :, None]
        w_west = harmonic(kappa, jnp.concatenate([leftside, kappa[:, :-1]], axis=1))[:, :, None]
        w_east = harmonic(kappa, jnp.concatenate([kappa[:, 1:], rightside], axis=1))[:, :, None]
        diagonal = w_north + w_south + w_west + w_east

        counts_all = lax.all_gather(coarse_counts, grid_axes, tiled=True)
        n_sub = counts_all.shape[0]
        starts = jnp.cumsum(counts_all) - counts_all
        slot = jnp.arange(n_sub * kmax)
        owner = slot // kmax
        column = slot % kmax
        target = jnp.where(column < counts_all[owner], starts[owner] + column, -1)
        pack_mat = (jnp.arange(ktot)[:, None] == target[None, :]).astype(jnp.float32)
        self_index = row_id * n_col + col_id
        own_slots = jnp.arange(kmax)
        own_target = jnp.where(own_slots < counts_all[self_index], starts[self_index] + own_slots, -1)
        pick_mat = (own_target[:, None] == jnp.arange(ktot)[None, :]).astype(jnp.float32)
        own_map = matmul(matmul(pick_mat, coarse_inv), pack_mat)

        def apply_local(field):
            from_top = lax.ppermute(field[-1:], 'sx', to_below)
            from_bottom = lax.ppermute(field[:1], 'sx', to_above)
            from_left = lax.ppermute(field[:, -1:], 'sy', to_right)
            from_right = lax.ppermute(field[:, :1], 'sy', to_left)
            north = jnp.concatenate([from_top, field[:-1]], axis=0)
            south = jnp.concatenate([field[1:], from_bottom], axis=0)
            west = jnp.concatenate([from_left, field[:, :-1]], axis=1)
            east = jnp.concatenate([field[:, 1:], from_right], axis=1)
            return diagonal * field - w_north * north - w_south * south - w_west * west - w_east * east

        def schwarz(resid):
            from_top = lax.ppermute(resid[size - over:], 'sx', to_below)
            from_bottom = lax.ppermute(resid[:over], 'sx', to_above)
            tall = jnp.concatenate([from_top, resid, from_bottom], axis=0)
            from_left = lax.ppermute(tall[:, size - over:], 'sy', to_right)
            from_right = lax.ppermute(tall[:, :over], 'sy', to_left)
            extended = jnp.concatenate([from_left, tall, from_right], axis=1)
            local = matmul(inverse, extended.reshape(edge * edge, n_rhs)).reshape(edge, edge, n_rhs)
            back_left = lax.ppermute(local[:, :over], 'sy', to_left)
            back_right = lax.ppermute(local[:, size + over:], 'sy', to_right)
            wide = (local[:, over:over + size] + jnp.pad(back_left, ((0, 0), (size - over, 0), (0, 0))) + jnp.pad(back_right, ((0, 0), (0, size - over), (0, 0))))
            back_up = lax.ppermute(wide[:over], 'sx', to_above)
            back_down = lax.ppermute(wide[size + over:], 'sx', to_below)
            level_one = (wide[over:over + size] + jnp.pad(back_up, ((size - over, 0), (0, 0), (0, 0))) + jnp.pad(back_down, ((0, size - over), (0, 0), (0, 0))))
            restrict = jnp.einsum('mk,mb->kb', basis, resid.reshape(size * size, n_rhs), precision=highest, preferred_element_type=jnp.float32)
            gathered = lax.all_gather(restrict, grid_axes, tiled=True)
            own_coef = matmul(own_map, gathered)
            return level_one + matmul(basis, own_coef).reshape(size, size, n_rhs)

        def global_dot(first, second):
            return lax.psum(jnp.sum(first * second, axis=(0, 1)), grid_axes)

        forcing_norm = jnp.sqrt(global_dot(forcing, forcing))
        solved = jnp.zeros_like(forcing)
        resid = forcing
        precond = schwarz(resid)
        direction = precond
        rz_dot = global_dot(resid, precond)
        norms = []
        for step in range(ITERS):
            image = apply_local(direction)
            alpha = rz_dot / global_dot(direction, image)
            solved = solved + alpha * direction
            resid = resid - alpha * image
            if step < ITERS - 1:
                precond = schwarz(resid)
                both = lax.psum(jnp.stack([jnp.sum(resid * precond, axis=(0, 1)), jnp.sum(resid * resid, axis=(0, 1))]), grid_axes)
                norms.append(jnp.sqrt(both[1]) / forcing_norm)
                direction = precond + (both[0] / rz_dot) * direction
                rz_dot = both[0]
            else:
                norms.append(jnp.sqrt(global_dot(resid, resid)) / forcing_norm)
        return solved, jnp.stack(norms)

    cell_spec = P(('batch', 'sx'), 'sy', None)
    sub_spec = P(('batch', 'sx', 'sy'), None, None)
    return jax.shard_map(body, mesh=mesh, in_specs=(cell_spec, P(('batch', 'sx'), 'sy'), sub_spec, sub_spec, P(('batch', 'sx', 'sy')), P('batch', None)), out_specs=(cell_spec, P('batch', None)), check_vma=False)
```

profile of v0, /device:TPU:97, one launch (start us, length us, event | category | flops | bytes accessed | tf_op | source)
XLA Modules:
  0.0 1783.5 jit_solution(2540723671873876274)
XLA Ops:
  16.8 47.3 %all-reduce.32 = s32[32]{0:T(128)S(1)} all-reduce(s32[32]{0:T(128)S(1)} %dynamic-update-slice), channel_id=1, replica_groups=mesh['batch'=1,'sy'=4,'sx'=8] {'sx','sy'}, use_global_device_ids=true, to_apply=%add.32 | all-reduce | flops 32 | bytes 256
  109.6 31.1 %compare_select_fusion.13 = s32[256]{0:T(256)S(1)} fusion(pred[256]{0:T(512)(128)(4,1)S(1)} %compare_reduce_fusion, pred[256]{0:T(512)(128)(4,1)S(1)} %compare_reduce_fusion.1, pred[256]{0:T(512)(128)(4,1)S(1)} %compare_reduce_fusion.2, pred[256]{0:T(512)(128)(4,1)S(1)} %compare_reduce_fusion.3, pred[256]{0:T(512)(128)(4,1)S(1)} %compare_reduce_fusion.4, ...), kind=kLoop, calls=%fused_computation.298 | loop fusion | flops 15104 | bytes 9672 | tf_op jit(solution)/shard_map/jit(_where)/select_n | solution.py:59
  226.7 45.9 %all-reduce.34 = (f32[192]{0:T(256)S(1)}, f32[192]{0:T(256)S(1)}) all-reduce(f32[192]{0:T(256)S(1)} %get-tuple-element.3, f32[192]{0:T(256)S(1)} %get-tuple-element.4), channel_id=1, replica_groups=mesh['batch'=1,'sy'=4,'sx'=8] {'sx','sy'}, use_global_device_ids=true, to_apply=%region_2.3 | all-reduce | flops 384 | bytes 3072 | tf_op jit(solution)/shard_map/psum | solution.py:98
  286.7 28.2 %all_gather.29 = f32[256,192]{1,0:T(8,128)} all-gather(f32[8,192]{1,0:T(8,128)S(1)} %convolution_bitcast_fusion.14), channel_id=1, replica_groups=mesh['batch'=1,'sy'=4,'sx'=8] {'sx','sy'}, dimensions={0}, use_global_device_ids=true | all-gather | bytes 202752 | tf_op jit(solution)/shard_map/all_gather | solution.py:93
  369.4 45.7 %psum.128 = f32[2,192]{1,0:T(2,128)S(1)} all-reduce(f32[2,192]{1,0:T(2,128)S(1)} %pad_maximum_fusion.33), channel_id=1, replica_groups=mesh['batch'=1,'sy'=4,'sx'=8] {'sx','sy'}, use_global_device_ids=true, to_apply=%region_7.8 | all-reduce | flops 384 | bytes 3072 | tf_op jit(solution)/shard_map/psum | solution.py:114
  430.8 46.0 %psum.129 = f32[192]{0:T(256)S(1)} all-reduce(f32[192]{0:T(256)S(1)} %get-tuple-element.35), channel_id=1, replica_groups=mesh['batch'=1,'sy'=4,'sx'=8] {'sx','sy'}, use_global_device_ids=true, to_apply=%region_9.10 | all-reduce | flops 192 | bytes 1536 | tf_op jit(solution)/shard_map/psum | solution.py:98
  578.3 45.0 %psum.130 = f32[2,192]{1,0:T(2,128)S(1)} all-reduce(f32[2,192]{1,0:T(2,128)S(1)} %pad_maximum_fusion.34), channel_id=1, replica_groups=mesh['batch'=1,'sy'=4,'sx'=8] {'sx','sy'}, use_global_device_ids=true, to_apply=%region_12.13 | all-reduce | flops 384 | bytes 3072 | tf_op jit(solution)/shard_map/psum | solution.py:114
  639.3 46.6 %psum.131 = f32[192]{0:T(256)S(1)} all-reduce(f32[192]{0:T(256)S(1)} %get-tuple-element.33), channel_id=1, replica_groups=mesh['batch'=1,'sy'=4,'sx'=8] {'sx','sy'}, use_global_device_ids=true, to_apply=%region_14.15 | all-reduce | flops 192 | bytes 1536 | tf_op jit(solution)/shard_map/psum | solution.py:98
  700.3 28.3 %all_gather.31 = f32[256,192]{1,0:T(8,128)S(1)} all-gather(f32[8,192]{1,0:T(8,128)S(1)} %convolution_bitcast_fusion.12), channel_id=1, replica_groups=mesh['batch'=1,'sy'=4,'sx'=8] {'sx','sy'}, dimensions={0}, use_global_device_ids=true | all-gather | bytes 202752 | tf_op jit(solution)/shard_map/all_gather | solution.py:93
  787.3 45.4 %psum.132 = f32[2,192]{1,0:T(2,128)S(1)} all-reduce(f32[2,192]{1,0:T(2,128)S(1)} %pad_maximum_fusion.35), channel_id=1, replica_groups=mesh['batch'=1,'sy'=4,'sx'=8] {'sx','sy'}, use_global_device_ids=true, to_apply=%region_17.18 | all-reduce | flops 384 | bytes 3072 | tf_op jit(solution)/shard_map/psum | solution.py:114
  848.2 46.6 %psum.133 = f32[192]{0:T(256)S(1)} all-reduce(f32[192]{0:T(256)S(1)} %get-tuple-element.31), channel_id=1, replica_groups=mesh['batch'=1,'sy'=4,'sx'=8] {'sx','sy'}, use_global_device_ids=true, to_apply=%region_19.20 | all-reduce | flops 192 | bytes 1536 | tf_op jit(solution)/shard_map/psum | solution.py:98
  909.5 28.0 %all_gather.32 = f32[256,192]{1,0:T(8,128)S(1)} all-gather(f32[8,192]{1,0:T(8,128)S(1)} %convolution_bitcast_fusion.11), channel_id=1, replica_groups=mesh['batch'=1,'sy'=4,'sx'=8] {'sx','sy'}, dimensions={0}, use_global_device_ids=true | all-gather | bytes 202752 | tf_op jit(solution)/shard_map/all_gather | solution.py:93
  996.4 45.1 %psum.134 = f32[2,192]{1,0:T(2,128)S(1)} all-reduce(f32[2,192]{1,0:T(2,128)S(1)} %pad_maximum_fusion.36), channel_id=1, replica_groups=mesh['batch'=1,'sy'=4,'sx'=8] {'sx','sy'}, use_global_device_ids=true, to_apply=%region_22.23 | all-reduce | flops 384 | bytes 3072 | tf_op jit(solution)/shard_map/psum | solution.py:114
  1057.6 46.6 %psum.135 = f32[192]{0:T(256)S(1)} all-reduce(f32[192]{0:T(256)S(1)} %get-tuple-element.29), channel_id=1, replica_groups=mesh['batch'=1,'sy'=4,'sx'=8] {'sx','sy'}, use_global_device_ids=true, to_apply=%region_24.25 | all-reduce | flops 192 | bytes 1536 | tf_op jit(solution)/shard_map/psum | solution.py:98
  1118.7 28.3 %all_gather.33 = f32[256,192]{1,0:T(8,128)S(1)} all-gather(f32[8,192]{1,0:T(8,128)S(1)} %convolution_bitcast_fusion.10), channel_id=1, replica_groups=mesh['batch'=1,'sy'=4,'sx'=8] {'sx','sy'}, dimensions={0}, use_global_device_ids=true | all-gather | bytes 202752 | tf_op jit(solution)/shard_map/all_gather | solution.py:93
  1205.6 45.4 %psum.136 = f32[2,192]{1,0:T(2,128)S(1)} all-reduce(f32[2,192]{1,0:T(2,128)S(1)} %pad_maximum_fusion.37), channel_id=1, replica_groups=mesh['batch'=1,'sy'=4,'sx'=8] {'sx','sy'}, use_global_device_ids=true, to_apply=%region_27.28 | all-reduce | flops 384 | bytes 3072 | tf_op jit(solution)/shard_map/psum | solution.py:114
  1266.9 46.6 %psum.137 = f32[192]{0:T(256)S(1)} all-reduce(f32[192]{0:T(256)S(1)} %get-tuple-element.27), channel_id=1, replica_groups=mesh['batch'=1,'sy'=4,'sx'=8] {'sx','sy'}, use_global_device_ids=true, to_apply=%region_29.30 | all-reduce | flops 192 | bytes 1536 | tf_op jit(solution)/shard_map/psum | solution.py:98
  1328.2 28.0 %all_gather.34 = f32[256,192]{1,0:T(8,128)S(1)} all-gather(f32[8,192]{1,0:T(8,128)S(1)} %convolution_bitcast_fusion.9), channel_id=1, replica_groups=mesh['batch'=1,'sy'=4,'sx'=8] {'sx','sy'}, dimensions={0}, use_global_device_ids=true | all-gather | bytes 202752 | tf_op jit(solution)/shard_map/all_gather | solution.py:93
  1415.2 45.0 %psum.138 = f32[2,192]{1,0:T(2,128)} all-reduce(f32[2,192]{1,0:T(2,128)S(1)} %pad_maximum_fusion.38), channel_id=1, replica_groups=mesh['batch'=1,'sy'=4,'sx'=8] {'sx','sy'}, use_global_device_ids=true, to_apply=%region_32.33 | all-reduce | flops 384 | bytes 3072 | tf_op jit(solution)/shard_map/psum | solution.py:114
  1477.3 46.7 %psum.139 = f32[192]{0:T(256)S(1)} all-reduce(f32[192]{0:T(256)S(1)} %get-tuple-element.25), channel_id=1, replica_groups=mesh['batch'=1,'sy'=4,'sx'=8] {'sx','sy'}, use_global_device_ids=true, to_apply=%region_34.35 | all-reduce | flops 192 | bytes 1536 | tf_op jit(solution)/shard_map/psum | solution.py:98
  1538.4 28.2 %all_gather.35 = f32[256,192]{1,0:T(8,128)S(1)} all-gather(f32[8,192]{1,0:T(8,128)S(1)} %convolution_bitcast_fusion.8), channel_id=1, replica_groups=mesh['batch'=1,'sy'=4,'sx'=8] {'sx','sy'}, dimensions={0}, use_global_device_ids=true | all-gather | bytes 202752 | tf_op jit(solution)/shard_map/all_gather | solution.py:93
  1625.0 45.7 %psum.140 = f32[2,192]{1,0:T(2,128)S(1)} all-reduce(f32[2,192]{1,0:T(2,128)S(1)} %pad_maximum_fusion.39), channel_id=1, replica_groups=mesh['batch'=1,'sy'=4,'sx'=8] {'sx','sy'}, use_global_device_ids=true, to_apply=%region_37.38 | all-reduce | flops 384 | bytes 3072 | tf_op jit(solution)/shard_map/psum | solution.py:114
  1686.1 46.5 %psum.141 = f32[192]{0:T(256)S(1)} all-reduce(f32[192]{0:T(256)S(1)} %get-tuple-element.23), channel_id=1, replica_groups=mesh['batch'=1,'sy'=4,'sx'=8] {'sx','sy'}, use_global_device_ids=true, to_apply=%region_39.40 | all-reduce | flops 192 | bytes 1536 | tf_op jit(solution)/shard_map/psum | solution.py:98
  1737.8 44.6 %all-reduce.33 = (f32[192]{0:T(256)S(1)}, f32[192]{0:T(256)S(1)}) all-reduce(f32[192]{0:T(256)S(1)} %copy-done.32, f32[192]{0:T(256)S(1)} %get-tuple-element.201), channel_id=1, replica_groups=mesh['batch'=1,'sy'=4,'sx'=8] {'sx','sy'}, use_global_device_ids=true, to_apply=%region_41.42 | all-reduce | flops 384 | bytes 3072 | tf_op jit(solution)/shard_map/psum | solution.py:98
  (522 shorter events, 798.8 us)
Async XLA Ops:
  1.4 141.9 %collective-permute-start.9 = (f32[1,32]{1,0:T(1,128)S(1)}, f32[1,32]{1,0:T(1,128)S(1)}, u32[]{:S(2)}, u32[]{:S(2)}) collective-permute-start(f32[1,32]{1,0:T(1,128)S(1)} %slice.519), channel_id=1, source_target_pairs={{1,0},{2,1},{3,2},{4,3},{5,4},{6,5},{7,6},{9,8},{10,9},{11,10},{12... | collective-permute-start | bytes 392 | tf_op jit(solution)/shard_map/ppermute | solution.py:40
  5.3 146.7 %collective-permute-start.11 = (f32[32,1]{1,0:T(8,128)}, f32[32,1]{1,0:T(8,128)S(1)}, u32[]{:S(2)}, u32[]{:S(2)}) collective-permute-start(f32[32,1]{1,0:T(8,128)} %bitcast.340), channel_id=1, source_target_pairs={{8,0},{16,8},{24,16},{9,1},{17,9},{25,17},{10,2},{18,10},{26,18},{... | collective-permute-start | bytes 392 | tf_op jit(solution)/shard_map/ppermute | solution.py:42
  7.7 146.6 %collective-permute-start.1 = (f32[4,32,192]{2,1,0:T(8,128)S(1)}, f32[4,32,192]{2,1,0:T(8,128)S(1)}, u32[]{:S(2)}, u32[]{:S(2)}) collective-permute-start(f32[4,32,192]{2,1,0:T(8,128)S(1)} %get-tuple-element.169), channel_id=1, source_target_pairs={{1,0},{2,1},{3,2},{4,3},{5,4},{6,5},{7,6},{9,8},{10,9},{11,10},{12... | collective-permute-start | bytes 294920 | tf_op jit(solution)/shard_map/ppermute | solution.py:80
  9.6 144.5 %collective-permute-start = (f32[4,32,192]{2,1,0:T(8,128)S(1)}, f32[4,32,192]{2,1,0:T(8,128)S(1)}, u32[]{:S(2)}, u32[]{:S(2)}) collective-permute-start(f32[4,32,192]{2,1,0:T(8,128)S(1)} %get-tuple-element.170), channel_id=1, source_target_pairs={{0,1},{1,2},{2,3},{3,4},{4,5},{5,6},{6,7},{8,9},{9,10},{10,11},{11... | collective-permute-start | bytes 294920 | tf_op jit(solution)/shard_map/ppermute | solution.py:79
  143.3 54.3 %collective-permute-start.8 = (f32[1,32]{1,0:T(1,128)S(1)}, f32[1,32]{1,0:T(1,128)S(1)}, u32[]{:S(2)}, u32[]{:S(2)}) collective-permute-start(f32[1,32]{1,0:T(1,128)S(1)} %get-tuple-element.178), channel_id=1, source_target_pairs={{0,1},{1,2},{2,3},{3,4},{4,5},{5,6},{6,7},{8,9},{9,10},{10,11},{11... | collective-permute-start | bytes 392 | tf_op jit(solution)/shard_map/ppermute | solution.py:39
  282.9 32.0 %collective-permute-start.18 = (f32[40,4,192]{2,1,0:T(4,128)S(1)}, f32[40,4,192]{2,1,0:T(4,128)S(1)}, u32[]{:S(2)}, u32[]{:S(2)}) collective-permute-start(f32[40,4,192]{2,1,0:T(4,128)S(1)} %get-tuple-element.85), channel_id=1, source_target_pairs={{0,8},{8,16},{16,24},{1,9},{9,17},{17,25},{2,10},{10,18},{18,26},{... | collective-permute-start | bytes 368648 | tf_op jit(solution)/shard_map/ppermute | solution.py:82
  284.8 30.1 %collective-permute-start.19 = (f32[40,4,192]{2,1,0:T(4,128)S(1)}, f32[40,4,192]{2,1,0:T(4,128)S(1)}, u32[]{:S(2)}, u32[]{:S(2)}) collective-permute-start(f32[40,4,192]{2,1,0:T(4,128)S(1)} %get-tuple-element.86), channel_id=1, source_target_pairs={{8,0},{16,8},{24,16},{9,1},{17,9},{25,17},{10,2},{18,10},{26,18},{... | collective-permute-start | bytes 368648 | tf_op jit(solution)/shard_map/ppermute | solution.py:83
  488.5 31.2 %collective-permute-start.30 = (f32[40,4,192]{2,1,0:T(4,128)S(1)}, f32[40,4,192]{2,1,0:T(4,128)S(1)}, u32[]{:S(2)}, u32[]{:S(2)}) collective-permute-start(f32[40,4,192]{2,1,0:T(4,128)S(1)} %get-tuple-element.81), channel_id=1, source_target_pairs={{0,8},{8,16},{16,24},{1,9},{9,17},{17,25},{2,10},{10,18},{18,26},{... | collective-permute-start | bytes 368648 | tf_op jit(solution)/shard_map/ppermute | solution.py:82
  489.8 29.9 %collective-permute-start.31 = (f32[40,4,192]{2,1,0:T(4,128)S(1)}, f32[40,4,192]{2,1,0:T(4,128)S(1)}, u32[]{:S(2)}, u32[]{:S(2)}) collective-permute-start(f32[40,4,192]{2,1,0:T(4,128)S(1)} %get-tuple-element.82), channel_id=1, source_target_pairs={{8,0},{16,8},{24,16},{9,1},{17,9},{25,17},{10,2},{18,10},{26,18},{... | collective-permute-start | bytes 368648 | tf_op jit(solution)/shard_map/ppermute | solution.py:83
  560.0 16.5 collective-permute-start.34
  697.0 31.6 %collective-permute-start.42 = (f32[40,4,192]{2,1,0:T(4,128)S(1)}, f32[40,4,192]{2,1,0:T(4,128)S(1)}, u32[]{:S(2)}, u32[]{:S(2)}) collective-permute-start(f32[40,4,192]{2,1,0:T(4,128)S(1)} %get-tuple-element.77), channel_id=1, source_target_pairs={{0,8},{8,16},{16,24},{1,9},{9,17},{17,25},{2,10},{10,18},{18,26},{... | collective-permute-start | bytes 368648 | tf_op jit(solution)/shard_map/ppermute | solution.py:82
  698.3 30.2 %collective-permute-start.43 = (f32[40,4,192]{2,1,0:T(4,128)S(1)}, f32[40,4,192]{2,1,0:T(4,128)S(1)}, u32[]{:S(2)}, u32[]{:S(2)}) collective-permute-start(f32[40,4,192]{2,1,0:T(4,128)S(1)} %get-tuple-element.78), channel_id=1, source_target_pairs={{8,0},{16,8},{24,16},{9,1},{17,9},{25,17},{10,2},{18,10},{26,18},{... | collective-permute-start | bytes 368648 | tf_op jit(solution)/shard_map/ppermute | solution.py:83
  768.9 16.1 collective-permute-start.46
  906.2 31.2 %collective-permute-start.54 = (f32[40,4,192]{2,1,0:T(4,128)S(1)}, f32[40,4,192]{2,1,0:T(4,128)S(1)}, u32[]{:S(2)}, u32[]{:S(2)}) collective-permute-start(f32[40,4,192]{2,1,0:T(4,128)S(1)} %get-tuple-element.73), channel_id=1, source_target_pairs={{0,8},{8,16},{16,24},{1,9},{9,17},{17,25},{2,10},{10,18},{18,26},{... | collective-permute-start | bytes 368648 | tf_op jit(solution)/shard_map/ppermute | solution.py:82
  907.6 29.9 %collective-permute-start.55 = (f32[40,4,192]{2,1,0:T(4,128)S(1)}, f32[40,4,192]{2,1,0:T(4,128)S(1)}, u32[]{:S(2)}, u32[]{:S(2)}) collective-permute-start(f32[40,4,192]{2,1,0:T(4,128)S(1)} %get-tuple-element.74), channel_id=1, source_target_pairs={{8,0},{16,8},{24,16},{9,1},{17,9},{25,17},{10,2},{18,10},{26,18},{... | collective-permute-start | bytes 368648 | tf_op jit(solution)/shard_map/ppermute | solution.py:83
  977.7 16.5 collective-permute-start.58
  1115.4 31.6 %collective-permute-start.66 = (f32[40,4,192]{2,1,0:T(4,128)S(1)}, f32[40,4,192]{2,1,0:T(4,128)S(1)}, u32[]{:S(2)}, u32[]{:S(2)}) collective-permute-start(f32[40,4,192]{2,1,0:T(4,128)S(1)} %get-tuple-element.69), channel_id=1, source_target_pairs={{0,8},{8,16},{16,24},{1,9},{9,17},{17,25},{2,10},{10,18},{18,26},{... | collective-permute-start | bytes 368648 | tf_op jit(solution)/shard_map/ppermute | solution.py:82
  1116.7 30.2 %collective-permute-start.67 = (f32[40,4,192]{2,1,0:T(4,128)S(1)}, f32[40,4,192]{2,1,0:T(4,128)S(1)}, u32[]{:S(2)}, u32[]{:S(2)}) collective-permute-start(f32[40,4,192]{2,1,0:T(4,128)S(1)} %get-tuple-element.70), channel_id=1, source_target_pairs={{8,0},{16,8},{24,16},{9,1},{17,9},{25,17},{10,2},{18,10},{26,18},{... | collective-permute-start | bytes 368648 | tf_op jit(solution)/shard_map/ppermute | solution.py:83
  1187.2 16.2 collective-permute-start.70
  1324.9 31.3 %collective-permute-start.78 = (f32[40,4,192]{2,1,0:T(4,128)S(1)}, f32[40,4,192]{2,1,0:T(4,128)S(1)}, u32[]{:S(2)}, u32[]{:S(2)}) collective-permute-start(f32[40,4,192]{2,1,0:T(4,128)S(1)} %get-tuple-element.65), channel_id=1, source_target_pairs={{0,8},{8,16},{16,24},{1,9},{9,17},{17,25},{2,10},{10,18},{18,26},{... | collective-permute-start | bytes 368648 | tf_op jit(solution)/shard_map/ppermute | solution.py:82
  1326.3 29.9 %collective-permute-start.79 = (f32[40,4,192]{2,1,0:T(4,128)S(1)}, f32[40,4,192]{2,1,0:T(4,128)S(1)}, u32[]{:S(2)}, u32[]{:S(2)}) collective-permute-start(f32[40,4,192]{2,1,0:T(4,128)S(1)} %get-tuple-element.66), channel_id=1, source_target_pairs={{8,0},{16,8},{24,16},{9,1},{17,9},{25,17},{10,2},{18,10},{26,18},{... | collective-permute-start | bytes 368648 | tf_op jit(solution)/shard_map/ppermute | solution.py:83
  1396.5 16.5 collective-permute-start.82
  1534.9 31.7 %collective-permute-start.90 = (f32[40,4,192]{2,1,0:T(4,128)S(1)}, f32[40,4,192]{2,1,0:T(4,128)S(1)}, u32[]{:S(2)}, u32[]{:S(2)}) collective-permute-start(f32[40,4,192]{2,1,0:T(4,128)S(1)} %get-tuple-element.61), channel_id=1, source_target_pairs={{0,8},{8,16},{16,24},{1,9},{9,17},{17,25},{2,10},{10,18},{18,26},{... | collective-permute-start | bytes 368648 | tf_op jit(solution)/shard_map/ppermute | solution.py:82
  1536.5 30.1 %collective-permute-start.91 = (f32[40,4,192]{2,1,0:T(4,128)S(1)}, f32[40,4,192]{2,1,0:T(4,128)S(1)}, u32[]{:S(2)}, u32[]{:S(2)}) collective-permute-start(f32[40,4,192]{2,1,0:T(4,128)S(1)} %get-tuple-element.62), channel_id=1, source_target_pairs={{8,0},{16,8},{24,16},{9,1},{17,9},{25,17},{10,2},{18,10},{26,18},{... | collective-permute-start | bytes 368648 | tf_op jit(solution)/shard_map/ppermute | solution.py:83
  (115 other events, 1750.2 us)
where the time goes:
time: 1800 us; the launch traced here: 1780 us
  blocking collectives  1000 us (56%)
  starting transfers between devices  282 us (16%)
  matrix products  219 us (12%)
  other arithmetic  119 us (7%)
  local copies, waits for them, and re-layouts  78.2 us (4%)
  waiting for transfers between devices  76.6 us (4%)
    psum x9, blocking collectives, global_dot(): return lax.psum(jnp.sum(first * second, axis=(0, 1)), grid_axes)  416 us
    psum x7, blocking collectives, body(): lax.psum(jnp.stack([jnp.sum(resid * precond, axis=(0, 1)), jnp.sum(resid...  317 us
    all_gather x8, blocking collectives, schwarz(): gathered = lax.all_gather(restrict, grid_axes, tiled=True)  224 us
    dot_general x26, matrix products, matmul(): jnp.dot(first, second, precision=highest, preferred_element_type=jnp.floa...  213 us
    ppermute x8, starting transfers between devices, schwarz(): back_up = lax.ppermute(wide[:over], 'sx', to_above)  70.8 us
    unnamed x1, blocking collectives  47.3 us
    dot_general x16, local copies, waits for them, and re-layouts, matmul(): jnp.dot(first, second, precision=highest, preferred_element_type=jnp.floa...  39.8 us
  transfers between devices with their start and end apart: 100, of which 34 were waited for; matrix products, arithmetic and copies ran while one was open for 7% of the time, Pallas kernels for 0%

commit v1 on v0

v1 whole, which is shorter than its diff:
```python
import math
import jax
import jax.numpy as jnp
from jax import lax
from jax.experimental import pallas as pl
from jax.experimental.pallas import tpu as pltpu
from jax.sharding import PartitionSpec as P

ITERS = 8
MESH = pl.DeviceIdType.MESH
F32 = jnp.float32
BF16 = jnp.bfloat16
DIRS = (('N', -1, 0), ('S', 1, 0), ('W', 0, -1), ('E', 0, 1), ('NW', -1, -1), ('NE', -1, 1), ('SW', 1, -1), ('SE', 1, 1))
OPP = (1, 0, 3, 2, 7, 6, 5, 4)
COMBOS = ((0, 0), (0, 1), (1, 0), (0, 2), (1, 1), (2, 0))
ONE, TWO, FOUR, SUB, LANES = 1, 2, 4, 8, 128
SLOT = 3 * SUB


def repeat(count, body, by=ONE):
    def several(i, _):
        for n in range(by):
            body(i * by + n)
        return 0
    lax.fori_loop(0, count // by, several, 0)


def split3(x):
    high = x.astype(BF16)
    rest = x - high.astype(F32)
    mid = rest.astype(BF16)
    low = (rest - mid.astype(F32)).astype(BF16)
    return high, mid, low


def dot(a, b):
    return jnp.dot(a, b, preferred_element_type=F32)


def dot_highest(a, b):
    return jnp.dot(a, b, precision=lax.Precision.HIGHEST, preferred_element_type=F32)


def make_kernel(n_row, n_col, size, over, n_rhs, kmax, ktot):
    edge = size + 2 * over
    own = size * size
    strip = over * size
    corner = over * over
    ext = edge * edge
    n_dev = n_row * n_col
    lo, hi = over, over + size
    msg = strip + size + 2 * over
    cmsg = corner + 2 * over
    batch1 = 4 * msg + 4 * cmsg
    rows_all = batch1 + own
    k_main = own + 4 * strip
    k_corner = 4 * corner
    ring = size + 8
    u_off = [0, msg, 2 * msg, 3 * msg] + [4 * msg + cmsg * i for i in range(4)]
    u_len = [msg] * 4 + [cmsg] * 4
    h_off = [strip, 0, 2 * strip, 3 * strip] + [4 * strip + corner * i for i in range(4)]
    h_len = [strip] * 4 + [corner] * 4
    halves = ((0, LANES), (LANES, n_rhs))
    tail = n_rhs - LANES
    n_chip = n_dev // TWO

    def packed(rows):
        left = -(-rows // (TWO * SUB)) * SUB
        return left, rows + left
    m_len = [packed(n)[ONE] for n in u_len]
    m_off = [sum(m_len[:k]) for k in range(8)]
    q_len = [packed(n)[ONE] for n in h_len]
    q_rank = (1, 0, 2, 3, 4, 5, 6, 7)
    q_off = [sum(q_len[j] for j in range(8) if q_rank[j] < q_rank[k]) for k in range(8)]
    tiles = [(c, min(c + 128, ext)) for c in range(0, ext, 128)]
    half_own = own // 2

    def kernel(f_hbm, kappa_ref, l_hbm, basis_t_ref, count_ref, cinv_ref,
               x_ref, norm_ref,
               nat, perm, stage, lp, lc, rp, rc, v, pack, h_out, halo, u, g_out, g_raw, g, r, p, s, ms, z, mc, ag, ags, cell_ref,
               coef, bcat, b_t, c_map, edges, pack_c, ring_v, cg, nb, scal, c32,
               l_sem, f_sem, e_send, e_recv, h_send, h_recv, g_send, g_recv, ag_send, ag_recv, fw_send, fw_recv):
        row_id = lax.axis_index('sx')
        col_id = lax.axis_index('sy')
        me = row_id * n_col + col_id
        parity = row_id % TWO
        my_slot = (row_id // TWO) * n_col + col_id

        def has(k):
            _, dr, dc = DIRS[k]
            ok = True
            for pos, step, count in ((row_id, dr, n_row), (col_id, dc, n_col)):
                if step < 0:
                    test = pos > 0
                elif step > 0:
                    test = pos < count - 1
                else:
                    continue
                ok = test if ok is True else jnp.logical_and(ok, test)
            return ok

        def there(k):
            return {'sx': row_id + DIRS[k][1], 'sy': col_id + DIRS[k][2]}

        exists = [has(k) for k in range(8)]

        def remote(src, dst, send, recv, k):
            return pltpu.make_async_remote_copy(src_ref=src, dst_ref=dst, send_sem=send, recv_sem=recv, device_id=there(k), device_id_type=MESH)

        def band_copy(j):
            lines = pl.ds(over * j, over)
            return pltpu.make_async_copy(l_hbm.at[lines], nat.at[lines], l_sem.at[j])
        for j in range(edge // over):
            band_copy(j).start()
        f_copy = pltpu.make_async_copy(f_hbm, v, f_sem.at[0])
        f_copy.start()
        r_copy = pltpu.make_async_copy(f_hbm, r, f_sem.at[1])
        r_copy.start()

        for ref in (halo, g_raw, g_out, ags, p, s, ms, z, x_ref):
            ref[...] = jnp.zeros_like(ref)
        for i in range(size):
            cell_ref[size * i:size * i + size, 0:LANES] = jnp.broadcast_to(kappa_ref[i:i + ONE, :], (LANES, size)).T
        for c in range(0, own, LANES):
            cell_ref[c:c + LANES, LANES:LANES + kmax] = basis_t_ref[:, c:c + LANES].T
        for i in range(size):
            pack_c[0, i:i + 1, :] = cell_ref[size * i:size * i + 1, :]
            pack_c[1, i:i + 1, :] = cell_ref[size * i + size - 1:size * i + size, :]
        edges[0] = cell_ref[0:size, :]
        edges[1] = cell_ref[own - size:own, :]
        edges[2] = pack_c[0]
        edges[3] = pack_c[1]

        barrier = pltpu.get_barrier_semaphore()

        for d in range(ONE, n_dev):
            peer = (me + d) % n_dev
            pl.semaphore_signal(barrier, inc=ONE, device_id={'sx': peer // n_col, 'sy': peer % n_col}, device_id_type=MESH)
        pl.semaphore_wait(barrier, n_dev - 1)

        edge_src = [cell_ref.at[pl.ds(0, size)], cell_ref.at[pl.ds(own - size, size)], pack_c.at[0], pack_c.at[1]]
        edge_copy = [remote(edge_src[k], edges.at[OPP[k]], e_send.at[k], e_recv.at[OPP[k]], k) for k in range(4)]
        edge_in = [remote(edge_src[k], edges.at[k], e_send.at[k], e_recv.at[k], k) for k in range(4)]
        for k in range(4):
            @pl.when(exists[k])
            def _(k=k):
                edge_copy[k].start()

        sub8 = lax.broadcasted_iota(jnp.int32, (8, n_rhs), 0)
        low4 = sub8 < 4

        def roll4(t):
            return pltpu.roll(t, 4, 0)

        def slices(ref, off, length):
            return [ref.at[pl.ds(off[k], length[k])] for k in range(8)]
        h_src, h_dst = slices(h_out, q_off, q_len), slices(halo, q_off, q_len)
        h_copy = [remote(h_src[k], h_dst[OPP[k]], h_send.at[k], h_recv.at[OPP[k]], k) for k in range(8)]
        h_in = [remote(h_src[k], h_dst[k], h_send.at[k], h_recv.at[k], k) for k in range(8)]
        g_src, g_dst = slices(g_out, m_off, m_len), slices(g_raw, m_off, m_len)
        g_copy = [remote(g_src[k], g_dst[OPP[k]], g_send.at[k], g_recv.at[OPP[k]], k) for k in range(8)]
        g_in = [remote(g_src[k], g_dst[k], g_send.at[k], g_recv.at[k], k) for k in range(8)]

        def pack_message(out, at, src, first, rows):
            left, _ = packed(rows)
            out[at:at + rows, :] = src[first:first + rows, 0:LANES]
            at = at + rows
            out[at:at + left, 0:tail] = src[first:first + left, LANES:n_rhs]
            out[at:at + rows - left, LANES - tail:LANES] = src[first + left:first + rows, LANES:n_rhs]

        def each(copies, what):
            for k in (4, 5, 6, 7, 2, 3, 0, 1):
                @pl.when(exists[k])
                def _(k=k):
                    if what == 'start':
                        copies[k].start()
                    elif what == 'recv':
                        copies[k].wait_recv()
                    else:
                        copies[k].wait_send()

        def own_slot(par):
            return ag.at[par, 0, pl.ds(pl.multiple_of(my_slot * SLOT, SUB), SLOT)]

        def ag_start(par):
            ag[par, 0, pl.ds(pl.multiple_of(my_slot * SLOT, SUB), SLOT), :] = ags[par]
            for d in range(ONE, n_chip):
                peer = (my_slot + d) % n_chip
                pltpu.make_async_remote_copy(
                    src_ref=ags.at[par], dst_ref=own_slot(par), send_sem=ag_send.at[par], recv_sem=ag_recv.at[par],
                    device_id={'sx': TWO * (peer // n_col) + parity, 'sy': peer % n_col}, device_id_type=MESH).start()

        def ag_wait(par, sem):
            many = ag.at[par, 0, pl.ds(0, (n_chip - ONE) * SLOT)]
            pltpu.make_async_copy(many, many, sem.at[par]).wait()

        def forward(par):
            return pltpu.make_async_remote_copy(
                src_ref=ag.at[par, 0], dst_ref=ag.at[par, ONE], send_sem=fw_send.at[par], recv_sem=fw_recv.at[par],
                device_id={'sx': row_id + ONE - TWO * parity}, device_id_type=MESH)

        def ag_forward(par):
            ag_wait(par, ag_recv)
            forward(par).start()

        def ag_done(par):
            ag_wait(par, ag_send)
            forward(par).wait_send()

        def rows_sum(t):
            return jnp.sum(t, axis=0, keepdims=True)

        def pack_sides():
            for q in range(size // TWO):
                for c0, c1 in halves:
                    a, b = TWO * q * size, (TWO * q + ONE) * size
                    m = low4[:, :c1 - c0]
                    pack[0, SUB * q:SUB * q + SUB, c0:c1] = jnp.where(m, v[a:a + SUB, c0:c1], roll4(v[b:b + SUB, c0:c1]))
                    a, b = b - SUB, b + size - SUB
                    pack[ONE, SUB * q:SUB * q + SUB, c0:c1] = jnp.where(m, roll4(v[a:a + SUB, c0:c1]), v[b:b + SUB, c0:c1])
            sides = (pack.at[0], pack.at[ONE])
            for k, (src, first) in enumerate(((v, 0), (v, own - strip), (sides[0], 0), (sides[ONE], 0), (sides[0], 0), (sides[ONE], 0),
                                              (sides[0], strip - corner), (sides[ONE], strip - corner))):
                pack_message(h_out, q_off[k], src, first, h_len[k])

        f_copy.wait()
        r_copy.wait()
        pack_sides()
        each(h_copy, 'start')

        bt = split3(basis_t_ref[...])
        for i in range(3):
            c32[8 * i:8 * i + 8, :] = bt[i].astype(F32)
        b_t[...] = c32[...].astype(BF16)

        def split_own(i):
            rows = pl.ds(pl.multiple_of(i * size, size), size)
            parts = split3(v[rows, :])
            for j in range(3):
                rp[j, rows, :] = parts[j]
        repeat(size, split_own, FOUR)

        def restrict(par):
            d1 = dot(b_t[...], rp[0, 0:own, :])
            d2 = dot(b_t[0:16, :], rp[1, 0:own, :])
            d3 = dot(b_t[0:16, :], rp[2, 0:own, :])
            d = (d1[16:24] + d2[8:16] + d3[0:8]) + (d1[8:16] + d2[0:8]) + d1[0:8]
            ags[par, SUB:TWO * SUB, :] = d[:, 0:LANES]
            ags[par, TWO * SUB:SLOT, 0:tail] = d[:, LANES:n_rhs]

        restrict(0)
        ags[0, 0:ONE, :] = count_ref[0:ONE, :]
        ag_start(0)

        for k in range(4):
            @pl.when(exists[k])
            def _(k=k):
                edge_in[k].wait_recv()
                edge_copy[k].wait_send()

        def turn(count, col):
            for c0, c1 in tiles:
                turned = stage[0:count, c0:c1].T
                for n in range(c0, c1, 8):
                    perm[n // edge, n % edge:n % edge + 8, pl.ds(col, count)] = turned[n - c0:n - c0 + 8]

        def turn_band(jj):
            band_copy(jj).wait()
            for i in range(over):
                stage[size * i:size * i + size, :] = nat[over * jj + i, lo:hi, :]
            block = (jj + size // over + 1) % (size // over + 2)
            turn(strip, pl.multiple_of(block * strip, strip))
        repeat(edge // over, turn_band)
        for side, b0 in ((0, 0), (1, hi)):
            for i in range(size):
                stage[over * i:over * i + over, :] = nat[lo + i, b0:b0 + over, :]
            turn(strip, own + 2 * strip + side * strip)
        for q, (a0, b0) in enumerate(((0, 0), (0, hi), (hi, 0), (hi, hi))):
            for i in range(over):
                stage[corner * q + over * i:corner * q + over * i + over, :] = nat[a0 + i, b0:b0 + over, :]
        turn(k_corner, k_main)

        def put_parts(rows, x, xc):
            parts = split3(x)
            for j in range(3):
                lp[j, rows, :] = parts[j]
            c = [t.astype(F32) for t in split3(xc)]
            order = (c[0], c[0], c[0], c[1], c[1], c[2])
            lc[rows, :] = jnp.concatenate(order, axis=1).astype(BF16)

        def put_own(i):
            rows = pl.ds(pl.multiple_of(batch1 + i * size, size), size)
            put_parts(rows, perm[lo + i, lo:hi, 0:k_main], perm[lo + i, lo:hi, k_main:ext])
        repeat(size, put_own)

        def take(at, a0, na, b0, nb_):
            for i in range(na):
                stage[at + nb_ * i:at + nb_ * i + nb_, :] = perm[a0 + i, b0:b0 + nb_, :]
            return at + na * nb_

        def take_col(at, a0, na, b):
            for i in range(na):
                stage[at + i:at + i + 1, :] = perm[a0 + i, b:b + 1, :]
            return at + na

        def flush(count, first):
            step = 48

            def go(i):
                src = pl.ds(pl.multiple_of(i * step, step), step)
                dst = pl.ds(pl.multiple_of(first + i * step, step), step)
                put_parts(dst, stage[src, 0:k_main], stage[src, k_main:ext])
            repeat(count // step, go)

        at = 0
        for a_strip, a_own in ((0, lo), (hi, hi - 1)):
            at = take(at, a_strip, over, lo, size)
            at = take(at, a_own, 1, lo, size)
            at = take_col(at, a_strip, over, lo - 1)
            at = take_col(at, a_strip, over, hi)
        flush(at, 0)
        at = 0
        for b_strip, b_own in ((0, lo), (hi, hi - 1)):
            at = take(at, lo, size, b_strip, over)
            at = take_col(at, lo, size, b_own)
            at = take(at, lo - 1, 1, b_strip, over)
            at = take(at, hi, 1, b_strip, over)
        flush(at, 2 * msg)
        at = 0
        for a_strip, a_own in ((0, lo), (hi, hi - 1)):
            for b_strip, b_own in ((0, lo), (hi, hi - 1)):
                at = take(at, a_strip, over, b_strip, over)
                at = take(at, a_own, 1, b_strip, over)
                at = take_col(at, a_strip, over, b_own)
        flush(at, 4 * msg)

        k5 = 5 * kmax

        def put_basis(i, first, x):
            parts = [t.astype(F32) for t in split3(x)]
            perm[i, 0:size, 0:256] = jnp.zeros((size, 256), F32)
            for c, (j, _) in enumerate(COMBOS):
                perm[i, 0:size, k5 * c + first:k5 * c + first + kmax] = parts[j]
            bcat[pl.ds(pl.multiple_of(i * size, size), size), :] = perm[i, 0:size, 0:256].astype(BF16)

        def put_basis_line(i):
            put_basis(i, 0, cell_ref[pl.ds(pl.multiple_of(i * size, size), size), LANES:LANES + kmax])
        repeat(size, put_basis_line, TWO)
        for k in range(4):
            put_basis(size + k, kmax * (k + 1), edges[k, :, LANES:LANES + kmax])
        coef[...] = jnp.zeros_like(coef)

        width = LANES
        sub_k = lax.broadcasted_iota(jnp.int32, (8, width), 0)
        for i in range(size):
            perm[i, 0:size, 0:width] = cell_ref[size * i:size * i + size, 0:width]
            perm[i, size:ring, 0:width] = jnp.where(sub_k == 0, edges[3, i:i + 1, 0:width], edges[2, i:i + 1, 0:width])
        perm[size, 0:size, 0:width] = edges[1, :, 0:width]
        perm[size + 1, 0:size, 0:width] = edges[0, :, 0:width]
        wn, ws, ww, we, wd = range(5)

        def harmonic(a, b):
            return 2.0 * a * b / (a + b)

        def put_weights(i):
            rows = pl.ds(pl.multiple_of(i * size, size), size)
            mid = perm[i, 0:ring, 0:width]
            up = perm[(i + size + 1) % (size + 2), 0:size, 0:width]
            down = perm[i + 1, 0:size, 0:width]
            here = mid[0:size]
            a = harmonic(here, up)
            b = harmonic(here, down)
            c = harmonic(here, pltpu.roll(mid, 1, 0)[0:size])
            d = harmonic(here, pltpu.roll(mid, ring - 1, 0)[0:size])
            scal[wn, rows, :] = a
            scal[ws, rows, :] = b
            scal[ww, rows, :] = c
            scal[we, rows, :] = d
            scal[wd, rows, :] = a + b + c + d
        repeat(size, put_weights, FOUR)

        ag_forward(0)
        forward(0).wait_recv()
        n_slot = n_dev * SLOT
        dev_rows = ag[0].reshape(n_dev, SLOT, LANES)[:, 0:ONE, 0:SUB]
        count_row = jnp.broadcast_to(dev_rows, (n_dev, SLOT, SUB)).reshape(n_slot, SUB).T
        count_dev = jnp.broadcast_to(dev_rows, (n_dev, SUB, SUB)).reshape(n_dev * SUB, SUB).T

        def floor_div(a, b):
            return jnp.floor((a + 0.5) * (ONE / b))

        def slot_facts(shape, axis, step=ONE):
            at = lax.broadcasted_iota(jnp.int32, shape, axis).astype(F32) * float(step)
            slot = floor_div(at, SLOT)
            inside = at - slot * SLOT
            other = floor_div(slot, n_chip)
            chip = slot - other * n_chip
            line = floor_div(chip, n_col)
            mine = parity.astype(F32)
            odd = mine + other - TWO * mine * other
            return (TWO * line + odd) * n_col + (chip - line * n_col), inside
        sub_r, inside_r = slot_facts((n_dev * SUB, n_slot), 0, SLOT // SUB)
        sub_c, _ = slot_facts((n_dev * SUB, n_slot), ONE)
        before = jnp.where(jnp.logical_and(inside_r == 0.0, sub_r < sub_c), 1.0, 0.0).astype(F32)
        start_row = dot_highest(count_dev, before)
        _, place = slot_facts((SUB, n_slot), ONE)
        which = lax.broadcasted_iota(jnp.int32, (ktot, n_slot), 0).astype(F32)

        def one_hot(first):
            here = place - first
            target = jnp.where(jnp.logical_and(here >= 0.0, here < count_row), start_row + here, -1.0)
            return jnp.where(which == target[0:ONE, :], 1.0, 0.0).astype(F32)
        pack_low, pack_high = one_hot(SUB), one_hot(TWO * SUB)
        k_row = lax.broadcasted_iota(jnp.int32, (k5, n_slot), 0).astype(F32)
        block = floor_div(k_row, kmax)
        sub_k, inside_k = slot_facts((k5, n_slot), ONE)
        wanted = me.astype(F32) + jnp.zeros((k5, n_slot), F32)
        present = block == 0.0
        for k in range(4):
            shift = DIRS[k][1] * n_col + DIRS[k][2]
            wanted = wanted + jnp.where(block == k + ONE, float(shift), 0.0)
            present = jnp.logical_or(present, jnp.logical_and(block == k + ONE, exists[k]))
        chosen = jnp.logical_and(sub_k == wanted, inside_k == SUB + k_row - block * kmax)
        select = jnp.where(jnp.logical_and(chosen, present), 1.0, 0.0).astype(F32)
        pick = lax.dot_general(select, pack_low, (((1,), (1,)), ((), ())), precision=lax.Precision.HIGHEST, preferred_element_type=F32)
        pick = dot_highest(pick, cinv_ref[...])
        c_map[0:k5, :] = dot_highest(pick, pack_low)
        c_map[k5:TWO * k5, :] = dot_highest(pick, pack_high)

        def field(par):
            for h, (c0, c1) in enumerate(halves):
                w_ = c1 - c0

                def line(i, sums):
                    rows = pl.ds(pl.multiple_of(i * size, size), size)
                    mid = z[i, :, c0:c1]
                    here = mid[0:size]
                    up = z[(i + size + ONE) % (size + TWO), 0:size, c0:c1]
                    down = z[i + ONE, 0:size, c0:c1]
                    left = pltpu.roll(mid, ONE, 0)[0:size]
                    right = pltpu.roll(mid, ring - ONE, 0)[0:size]
                    out = (scal[wd, rows, 0:w_] * here - scal[wn, rows, 0:w_] * up - scal[ws, rows, 0:w_] * down
                           - scal[ww, rows, 0:w_] * left - scal[we, rows, 0:w_] * right)
                    v[rows, c0:c1] = out
                    parts = split3(out)
                    for j in range(3):
                        rp[j, rows, c0:c1] = parts[j]
                    res = r[rows, c0:c1]
                    new = []
                    for total, t in zip(sums, (res * here, here * out, here * s[rows, c0:c1], res * res)):
                        q = t[0:SUB]
                        for n in range(SUB, size, SUB):
                            q = q + t[n:n + SUB]
                        new.append(total + q)
                    return tuple(new)

                def lines(i, sums):
                    for n in range(FOUR):
                        sums = line(i * FOUR + n, sums)
                    return sums
                sums = lax.fori_loop(0, size // FOUR, lines, tuple(jnp.zeros((SUB, w_), F32) for _ in range(FOUR)))
                for n in range(FOUR):
                    ags[par, FOUR * h + n:FOUR * h + n + ONE, 0:w_] = rows_sum(sums[n])

        def totals(par):
            return jnp.sum(ag[par].reshape(n_dev, SLOT, LANES)[:, 0:SUB, :], axis=0)

        def products(rows, k0, k1):
            out = None
            for i, j in COMBOS:
                t = dot(lp[i, rows, k0:k1], rp[j, k0:k1, :])
                out = t if out is None else out + t
            return out

        def scalars(par, it):
            t = totals(par)
            for h, (c0, c1) in enumerate(halves):
                rz, zw, zs, rr = [t[FOUR * h + n:FOUR * h + n + ONE, 0:c1 - c0] for n in range(FOUR)]
                nb[it, :, c0:c1] = jnp.broadcast_to(rr, (SUB, c1 - c0))
                old_rz, old_pq = cg[0, 0:ONE, c0:c1], cg[ONE, 0:ONE, c0:c1]
                first = it <= ONE
                beta = jnp.where(first, 0.0, rz / old_rz)
                pq = zw + jnp.where(first, 0.0, 2.0 * beta * zs + beta * beta * old_pq)
                for n, value in enumerate((rz, pq, rz / pq, beta)):
                    cg[n, 0:ONE, c0:c1] = value

        def advance():
            for c0, c1 in halves:
                alpha = cg[TWO, 0:ONE, c0:c1]
                beta = cg[3, 0:ONE, c0:c1]

                def line(i):
                    rows = pl.ds(pl.multiple_of(i * size, size), size)
                    new_p = z[i, 0:size, c0:c1] + beta * p[rows, c0:c1]
                    new_s = v[rows, c0:c1] + beta * s[rows, c0:c1]
                    p[rows, c0:c1] = new_p
                    s[rows, c0:c1] = new_s
                    x_ref[rows, c0:c1] = x_ref[rows, c0:c1] + alpha * new_p
                    r[rows, c0:c1] = r[rows, c0:c1] - alpha * new_s
                repeat(size, line, TWO)

        gn, gs, gw, ge, gnw, gne, gsw, gse = u_off

        def fold():
            mine = batch1
            for k in range(8):
                first, rows, at = u_off[k], u_len[k], m_off[k]
                left, _ = packed(rows)
                g[first:first + rows, 0:LANES] = g_raw[at:at + rows, :]
                at = at + rows
                g[first:first + left, LANES:n_rhs] = g_raw[at:at + left, 0:tail]
                g[first + left:first + rows, LANES:n_rhs] = g_raw[at:at + rows - left, LANES - tail:LANES]
            u[mine:mine + strip, :] = u[mine:mine + strip, :] + g[gn:gn + strip, :]
            u[mine + own - strip:mine + own, :] = u[mine + own - strip:mine + own, :] + g[gs:gs + strip, :]
            for side, first, last in ((gw, gnw, gsw), (ge, gne, gse)):
                g[side:side + corner, :] = g[side:side + corner, :] + g[first:first + corner, :]
                end = side + strip
                g[end - corner:end, :] = g[end - corner:end, :] + g[last:last + corner, :]

            def last_rows(k):
                first = u_off[k] + u_len[k] - 8
                return g[first:first + 8, :]
            t = [last_rows(k) for k in range(8)]
            n_, s_, w_, e_, nw, ne, sw, se = t

            def lower(a):
                return jnp.where(low4, a, 0.0)

            def upper(a):
                return jnp.where(low4, 0.0, a)

            edge_sum = [
                (g[gn + strip:gn + strip + size, :] + u[gn + strip - size:gn + strip, :], lower(w_ + nw), upper(roll4(e_) + roll4(ne))),
                (g[gs + strip:gs + strip + size, :] + u[gs:gs + size, :], lower(roll4(w_) + sw), upper(e_ + roll4(se))),
                (g[gw + strip:gw + strip + size, :], lower(n_ + roll4(nw)), upper(roll4(s_) + sw)),
                (g[ge + strip:ge + strip + size, :], lower(roll4(n_) + roll4(ne)), upper(s_ + se)),
            ]
            for k in range(4):
                base, first, last = edge_sum[k]
                ring_v[k] = base + mc[own + size * k:own + size * k + size, :]
                ring_v[k, 0:8, :] = ring_v[k, 0:8, :] + first
                ring_v[k, size - 8:size, :] = ring_v[k, size - 8:size, :] + last

            for c0, c1 in halves:
                w = c1 - c0
                alpha = cg[TWO, 0:ONE, c0:c1]
                beta = cg[3, 0:ONE, c0:c1]
                sub = sub8[:, :w]
                low = low4[:, :w]
                at_w = jnp.logical_and(sub == 7, exists[2])
                at_e = jnp.logical_and(sub == 0, exists[3])

                def push(i, a, b, m):
                    new = m + beta * ms[i, a:b, c0:c1]
                    ms[i, a:b, c0:c1] = new
                    z[i, a:b, c0:c1] = z[i, a:b, c0:c1] - alpha * new

                def eight_lines(b):
                    tile = pl.ds(pl.multiple_of(8 * b, 8), 8)
                    ring_w = ring_v[2, tile, c0:c1]
                    ring_e = ring_v[3, tile, c0:c1]
                    for line in range(8):
                        i = 8 * b + line
                        odd = line % 2
                        four = 4 * (i - odd)
                        if not odd:
                            tw = g[pl.ds(pl.multiple_of(gw + four, 8), 8), c0:c1]
                            te = g[pl.ds(pl.multiple_of(ge + four, 8), 8), c0:c1]
                            uw = u[pl.ds(pl.multiple_of(gw + four, 8), 8), c0:c1]
                            ue = u[pl.ds(pl.multiple_of(ge + four, 8), 8), c0:c1]
                        base = pl.multiple_of(i * size, size)
                        add_w = jnp.where(low, roll4(tw) if odd else tw, 0.0)
                        add_e = jnp.where(low, 0.0, te if odd else roll4(te))
                        for n in range(0, size, 8):
                            m = u[pl.ds(mine + base + n, 8), c0:c1] + mc[pl.ds(base + n, 8), c0:c1]
                            if n == 0:
                                m = m + add_w
                            if n == size - 8:
                                m = m + add_e
                            push(i, n, n + 8, m)
                        own_w = (uw if odd else roll4(uw)) + ring_w[line:line + 1]
                        own_e = (roll4(ue) if odd else ue) + ring_e[line:line + 1]
                        push(i, size, ring, jnp.where(at_w, own_w, jnp.where(at_e, own_e, 0.0)))
                repeat(size // SUB, eight_lines)
                push(size, 0, size, jnp.where(exists[1], ring_v[1, :, c0:c1], 0.0))
                push(size + 1, 0, size, jnp.where(exists[0], ring_v[0, :, c0:c1], 0.0))

        cg[...] = jnp.zeros_like(cg)
        first_rows = pl.ds(0, batch1)
        part_a = pl.ds(batch1, half_own)
        part_b = pl.ds(batch1 + half_own, half_own)

        def iteration(it):
            par = it % 2

            @pl.when(it > 0)
            def _():
                field(par)
                pack_sides()
                each(h_copy, 'start')
                restrict(par)
                ag_start(par)

            u[first_rows, :] = products(first_rows, 0, own)
            u[part_a, :] = products(part_a, 0, own)
            each(h_in, 'recv')
            for k in range(8):
                rows, at = h_len[k], q_off[k]
                left, _ = packed(rows)
                upper = halo[at + rows:at + rows + left, :]
                low_parts = split3(halo[at:at + rows, :])
                high_parts = split3(jnp.concatenate([upper[:, 0:tail], upper[:, tail:LANES]], axis=0))
                if k < FOUR:
                    for j in range(3):
                        rp[j, own + h_off[k]:own + h_off[k] + rows, 0:LANES] = low_parts[j]
                        rp[j, own + h_off[k]:own + h_off[k] + rows, LANES:n_rhs] = high_parts[j]
                else:
                    for n, (_, j) in enumerate(COMBOS_C):
                        first = k_corner * n + h_off[k] - FOUR * strip
                        rc[first:first + rows, 0:LANES] = low_parts[j]
                        rc[first:first + rows, LANES:n_rhs] = high_parts[j]
            u[first_rows, :] = u[first_rows, :] + (products(first_rows, own, k_main) + dot(lc[first_rows, :], rc[...]))
            for k in range(8):
                pack_message(g_out, m_off[k], u, u_off[k], u_len[k])
            each(g_copy, 'start')
            u[part_a, :] = u[part_a, :] + (products(part_a, own, k_main) + dot(lc[part_a, :], rc[...]))

            @pl.when(it > 0)
            def _():
                ag_forward(par)
            u[part_b, :] = products(part_b, 0, k_main) + dot(lc[part_b, :], rc[...])

            @pl.when(it > 0)
            def _():
                forward(par).wait_recv()
                scalars(par, it)
                advance()

            @pl.when(it == 0)
            def _():
                cg[TWO, 0:ONE, :] = jnp.full((ONE, n_rhs), -1.0, F32)

            c = dot_highest(c_map[...], ag[par].reshape(n_slot, LANES))
            for (c0, c1), value in zip(halves, (c[0:k5], c[k5:TWO * k5, 0:tail])):
                parts = split3(value)
                for n, (_, j) in enumerate(COMBOS):
                    coef[k5 * n:k5 * n + k5, c0:c1] = parts[j].astype(F32)
            mc[...] = dot(bcat[...], coef[...].astype(BF16))
            each(g_in, 'recv')
            fold()
            each(h_copy, 'sent')
            each(g_copy, 'sent')
            ag_done(par)
        repeat(ITERS, iteration)

        this, last = ITERS % TWO, (ITERS + ONE) % TWO
        field(this)
        ag_start(this)
        ag_forward(this)
        forward(this).wait_recv()
        scalars(this, ITERS)
        advance()
        for h, (c0, c1) in enumerate(halves):
            def line(i, total):
                res = r[pl.ds(pl.multiple_of(i * size, size), size), c0:c1]
                t = res * res
                for n in range(0, size, SUB):
                    total = total + t[n:n + SUB]
                return total
            total = lax.fori_loop(0, size, line, jnp.zeros((SUB, c1 - c0), F32))
            ags[last, FOUR * h + 3:FOUR * h + FOUR, 0:c1 - c0] = rows_sum(total)
        ag_start(last)
        ag_forward(last)
        forward(last).wait_recv()
        t = totals(last)
        for h, (c0, c1) in enumerate(halves):
            nb[ITERS + ONE, :, c0:c1] = jnp.broadcast_to(t[FOUR * h + 3:FOUR * h + FOUR, 0:c1 - c0], (SUB, c1 - c0))
        base_norm = jnp.sqrt(nb[ONE])
        for k in range(ITERS):
            norm_ref[k:k + ONE, :] = (jnp.sqrt(nb[k + TWO]) / base_norm)[0:ONE]
        ag_done(this)
        ag_done(last)

    COMBOS_C = ((0, 0), (0, 1), (0, 2), (1, 0), (1, 1), (2, 0))
    scratch = [
        pltpu.VMEM((edge, edge, ext), F32),
        pltpu.VMEM((edge, edge, ext), F32),
        pltpu.VMEM((2 * msg, ext), F32),
        pltpu.VMEM((3, rows_all, k_main), BF16),
        pltpu.VMEM((rows_all, 6 * k_corner), BF16),
        pltpu.VMEM((3, k_main, n_rhs), BF16),
        pltpu.VMEM((6 * k_corner, n_rhs), BF16),
        pltpu.VMEM((own, n_rhs), F32),
        pltpu.VMEM((2, strip, n_rhs), F32),
        pltpu.VMEM((sum(q_len), LANES), F32),
        pltpu.VMEM((sum(q_len), LANES), F32),
        pltpu.VMEM((rows_all, n_rhs), F32),
        pltpu.VMEM((sum(m_len), LANES), F32),
        pltpu.VMEM((sum(m_len), LANES), F32),
        pltpu.VMEM((batch1, n_rhs), F32),
        pltpu.VMEM((own, n_rhs), F32),
        pltpu.VMEM((own, n_rhs), F32),
        pltpu.VMEM((own, n_rhs), F32),
        pltpu.VMEM((size + 2, ring, n_rhs), F32),
        pltpu.VMEM((size + 2, ring, n_rhs), F32),
        pltpu.VMEM((own + 4 * size, n_rhs), F32),
        pltpu.VMEM((TWO, TWO, n_chip * SLOT, LANES), F32),
        pltpu.VMEM((TWO, SLOT, LANES), F32),
        pltpu.VMEM((own, TWO * LANES), F32),
        pltpu.VMEM((256, n_rhs), F32),
        pltpu.VMEM((own + 4 * size, 256), BF16),
        pltpu.VMEM((3 * kmax, own), BF16),
        pltpu.VMEM((10 * kmax, n_dev * SLOT), F32),
        pltpu.VMEM((4, size, 256), F32),
        pltpu.VMEM((2, size, 256), F32),
        pltpu.VMEM((4, size, n_rhs), F32),
        pltpu.VMEM((4, SUB, n_rhs), F32),
        pltpu.VMEM((ITERS + 2, 8, n_rhs), F32),
        pltpu.VMEM((5, own, 128), F32),
        pltpu.VMEM((3 * kmax, own), F32),
        pltpu.SemaphoreType.DMA((edge // over,)),
        pltpu.SemaphoreType.DMA((2,)),
        pltpu.SemaphoreType.DMA((4,)), pltpu.SemaphoreType.DMA((4,)),
        pltpu.SemaphoreType.DMA((8,)), pltpu.SemaphoreType.DMA((8,)),
        pltpu.SemaphoreType.DMA((8,)), pltpu.SemaphoreType.DMA((8,)),
    ] + [pltpu.SemaphoreType.DMA((TWO,))] * 4

    return kernel, scratch


def solution(mesh):
    n_row = mesh.shape['sx']
    n_col = mesh.shape['sy']

    def body(forcing, kappa, local_inv, coarse_basis, coarse_counts, coarse_inv):
        size = forcing.shape[0]
        n_rhs = forcing.shape[2]
        edge = math.isqrt(local_inv.shape[1])
        over = (edge - size) // 2
        kmax = coarse_basis.shape[2]
        ktot = coarse_inv.shape[0]
        own = size * size
        count = jnp.broadcast_to(coarse_counts.astype(F32)[:, None], (SUB, LANES))
        kernel, scratch = make_kernel(n_row, n_col, size, over, n_rhs, kmax, ktot)
        vmem = pl.BlockSpec(memory_space=pltpu.VMEM)
        hbm = pl.BlockSpec(memory_space=pl.ANY)
        solved, norms = pl.pallas_call(
            kernel,
            out_shape=(jax.ShapeDtypeStruct((own, n_rhs), F32), jax.ShapeDtypeStruct((ITERS, n_rhs), F32)),
            in_specs=[hbm, vmem, hbm, vmem, vmem, vmem],
            out_specs=(vmem, vmem),
            scratch_shapes=scratch,
            compiler_params=pltpu.CompilerParams(collective_id=0, has_side_effects=True, vmem_limit_bytes=67043328),
        )(forcing.reshape(own, n_rhs), kappa, local_inv.reshape(edge, edge, edge * edge), coarse_basis[0].T, count, coarse_inv)
        return solved.reshape(size, size, n_rhs), norms

    cell_spec = P(('batch', 'sx'), 'sy', None)
    sub_spec = P(('batch', 'sx', 'sy'), None, None)
    return jax.shard_map(body, mesh=mesh, in_specs=(cell_spec, P(('batch', 'sx'), 'sy'), sub_spec, sub_spec, P(('batch', 'sx', 'sy')), P('batch', None)), out_specs=(cell_spec, P('batch', None)), check_vma=False)
```

time: 1800 us -> 209 us (0.12)
  blocking collectives: 1000 us -> 0 us
  starting transfers between devices: 282 us -> 0 us
  matrix products: 219 us -> 0 us
  Pallas kernels: 0 us -> 203 us
  other arithmetic: 119 us -> 0 us
  waiting for transfers between devices: 76.6 us -> 0 us
  local copies, waits for them, and re-layouts: 78.2 us -> 4.2 us
    psum x16 -> x0, blocking collectives: 733 us -> none  [the longest x9 416 us: global_dot(): return lax.psum(jnp.sum(first * second, axis=(0, 1)), grid_axes)]
    ppermute x100 -> x0, starting transfers between devices: 282 us -> none  [the longest x8 70.8 us: schwarz(): back_up = lax.ppermute(wide[:over], 'sx', to_above)]
    all_gather x8 -> x0, blocking collectives: 224 us -> none  [schwarz(): gathered = lax.all_gather(restrict, grid_axes, tiled=True)]
    dot_general x34 -> x0, matrix products: 219 us -> none  [the longest x26 213 us: matmul(): jnp.dot(first, second, precision=highest, preferred_element_type=jnp.floa...]
    pallas_call x0 -> x1, Pallas kernels: none -> 203 us  [body(): pl.pallas_call(kernel, out_shape=(jax.ShapeDtypeStruct((own, n_rhs), F32)...]
    ppermute x100 -> x0, waiting for transfers between devices: 76.6 us -> none  [the longest x8 30.4 us: schwarz(): from_bottom = lax.ppermute(resid[:over], 'sx', to_above)]
    unnamed x1 -> x0, blocking collectives: 47.3 us -> none
    dot_general x16 -> x0, local copies, waits for them, and re-layouts: 39.8 us -> none  [matmul(): jnp.dot(first, second, precision=highest, preferred_element_type=jnp.floa...]
  transfers between devices with their start and end apart: 100 -> 0, of which waited for: 34 -> 0; matrix products, arithmetic and copies ran while one was open for 7% -> 0% of each run, Pallas kernels for 0% -> 0%
where the time goes in v1:
time: 209 us
  Pallas kernels  203 us (97%)
  local copies, waits for them, and re-layouts  4.2 us (2%)
    pallas_call x1, Pallas kernels, body(): pl.pallas_call(kernel, out_shape=(jax.ShapeDtypeStruct((own, n_rhs), F32)...  203 us

profile of v1, /device:TPU:97, one launch (start us, length us, event | category | flops | bytes accessed | tf_op | source)
XLA Modules:
  0.0 208.6 jit_solution(9644988744001640067)
XLA Ops:
  1.3 0.6 broadcast_in_dim.9.count_ref
  1.9 203.1 %shard_map.77 = (f32[1024,192]{1,0:T(8,128)}, f32[8,192]{1,0:T(8,128)}) custom-call(f32[1024,192]{1,0:T(8,128)} %bitcast.9, f32[32,32]{1,0:T(8,128)} %kappa_ref.1, f32[40,40,1600]{2,1,0:T(8,128)} %bitcast.7, f32[8,1024]{1,0:T(8,128)} %bitcast.10, f32[8,128]{1,0:T(8,128)} %broadcast_in_dim.9.count_ref, f32[128,128]{1,0:T(8,128)} %cinv_ref.1), custom_call_target="tpu_custom_call" | custom-call | tf_op jit(solution)/shard_map/pallas_call | solution.py:747
  205.0 2.3 %copy.11 = f32[32,32,192]{2,1,0:T(8,128)} copy(f32[32,32,192]{2,1,0:T(8,128)} %bitcast.8) | data formatting | bytes 1572864
  207.3 1.3 copy.12

commit v2 on v1

--- a/solution.py
+++ b/solution.py
@@ -78,8 +78,8 @@
     def kernel(f_hbm, kappa_ref, l_hbm, basis_t_ref, count_ref, cinv_ref,
                x_ref, norm_ref,
                nat, perm, stage, lp, lc, rp, rc, v, pack, h_out, halo, u, g_out, g_raw, g, r, p, s, ms, z, mc, ag, ags, cell_ref,
-               coef, bcat, b_t, c_map, edges, pack_c, ring_v, cg, nb, scal, c32,
-               l_sem, f_sem, e_send, e_recv, h_send, h_recv, g_send, g_recv, ag_send, ag_recv, fw_send, fw_recv):
+               coef, bcat, b_t, c_map, edges, pack_c, ring_v, cg, nb, scal,
+               l_sem, f_sem, e_send, e_recv, h_send, h_recv, g_send, g_recv, ag_send, ag_recv, up_send, up_recv, fw_send, fw_recv):
         row_id = lax.axis_index('sx')
         col_id = lax.axis_index('sy')
         me = row_id * n_col + col_id
@@ -119,8 +119,10 @@
 
         for ref in (halo, g_raw, g_out, ags, p, s, ms, z, x_ref):
             ref[...] = jnp.zeros_like(ref)
+        eye = lax.broadcasted_iota(jnp.int32, (size, size), 0) == lax.broadcasted_iota(jnp.int32, (size, size), ONE)
         for i in range(size):
-            cell_ref[size * i:size * i + size, 0:LANES] = jnp.broadcast_to(kappa_ref[i:i + ONE, :], (LANES, size)).T
+            diagonal = jnp.where(eye, kappa_ref[i:i + ONE, :], 0.0)
+            cell_ref[size * i:size * i + size, 0:LANES] = jnp.broadcast_to(jnp.sum(diagonal, axis=ONE, keepdims=True), (size, LANES))
         for c in range(0, own, LANES):
             cell_ref[c:c + LANES, LANES:LANES + kmax] = basis_t_ref[:, c:c + LANES].T
         for i in range(size):
@@ -169,7 +171,7 @@
             out[at:at + rows - left, LANES - tail:LANES] = src[first + left:first + rows, LANES:n_rhs]
 
         def each(copies, what):
-            for k in (4, 5, 6, 7, 2, 3, 0, 1):
+            for k in (2, 3, 0, 1, 4, 5, 6, 7):
                 @pl.when(exists[k])
                 def _(k=k):
                     if what == 'start':
@@ -184,27 +186,35 @@
 
         def ag_start(par):
             ag[par, 0, pl.ds(pl.multiple_of(my_slot * SLOT, SUB), SLOT), :] = ags[par]
-            for d in range(ONE, n_chip):
-                peer = (my_slot + d) % n_chip
+            for d in range(ONE, n_col):
                 pltpu.make_async_remote_copy(
                     src_ref=ags.at[par], dst_ref=own_slot(par), send_sem=ag_send.at[par], recv_sem=ag_recv.at[par],
-                    device_id={'sx': TWO * (peer // n_col) + parity, 'sy': peer % n_col}, device_id_type=MESH).start()
-
-        def ag_wait(par, sem):
-            many = ag.at[par, 0, pl.ds(0, (n_chip - ONE) * SLOT)]
+                    device_id={'sy': (col_id + d) % n_col}, device_id_type=MESH).start()
+
+        def waits(par, sem, slots):
+            many = ag.at[par, 0, pl.ds(0, slots * SLOT)]
             pltpu.make_async_copy(many, many, sem.at[par]).wait()
+
+        def ag_second(par):
+            waits(par, ag_recv, n_col - ONE)
+            line = ag.at[par, 0, pl.ds(pl.multiple_of((row_id // TWO) * (n_col * SLOT), SUB), n_col * SLOT)]
+            for d in range(ONE, n_row // TWO):
+                pltpu.make_async_remote_copy(
+                    src_ref=line, dst_ref=line, send_sem=up_send.at[par], recv_sem=up_recv.at[par],
+                    device_id={'sx': (row_id + TWO * d) % n_row}, device_id_type=MESH).start()
 
         def forward(par):
             return pltpu.make_async_remote_copy(
                 src_ref=ag.at[par, 0], dst_ref=ag.at[par, ONE], send_sem=fw_send.at[par], recv_sem=fw_recv.at[par],
                 device_id={'sx': row_id + ONE - TWO * parity}, device_id_type=MESH)
 
-        def ag_forward(par):
-            ag_wait(par, ag_recv)
+        def ag_third(par):
+            waits(par, up_recv, n_chip - n_col)
             forward(par).start()
 
         def ag_done(par):
-            ag_wait(par, ag_send)
+            waits(par, ag_send, n_col - ONE)
+            waits(par, up_send, n_chip - n_col)
             forward(par).wait_send()
 
         def rows_sum(t):
@@ -229,15 +239,15 @@
         each(h_copy, 'start')
 
         bt = split3(basis_t_ref[...])
-        for i in range(3):
-            c32[8 * i:8 * i + 8, :] = bt[i].astype(F32)
-        b_t[...] = c32[...].astype(BF16)
+        for i, part in enumerate(bt):
+            stage[SUB * i:SUB * i + SUB, 0:own] = part.astype(F32)
+        b_t[...] = stage[0:SUB * len(bt), 0:own].astype(BF16)
 
         def split_own(i):
             rows = pl.ds(pl.multiple_of(i * size, size), size)
             parts = split3(v[rows, :])
-            for j in range(3):
-                rp[j, rows, :] = parts[j]
+            for j, part in enumerate(parts):
+                rp[j, rows, :] = part
         repeat(size, split_own, FOUR)
 
         def restrict(par):
@@ -257,6 +267,8 @@
             def _(k=k):
                 edge_in[k].wait_recv()
                 edge_copy[k].wait_send()
+
+        ag_second(0)
 
         def turn(count, col):
             for c0, c1 in tiles:
@@ -280,10 +292,12 @@
                 stage[corner * q + over * i:corner * q + over * i + over, :] = nat[a0 + i, b0:b0 + over, :]
         turn(k_corner, k_main)
 
+        ag_third(0)
+
         def put_parts(rows, x, xc):
             parts = split3(x)
-            for j in range(3):
-                lp[j, rows, :] = parts[j]
+            for j, part in enumerate(parts):
+                lp[j, rows, :] = part
             c = [t.astype(F32) for t in split3(xc)]
             order = (c[0], c[0], c[0], c[1], c[1], c[2])
             lc[rows, :] = jnp.concatenate(order, axis=1).astype(BF16)
@@ -379,7 +393,6 @@
             scal[wd, rows, :] = a + b + c + d
         repeat(size, put_weights, FOUR)
 
-        ag_forward(0)
         forward(0).wait_recv()
         n_slot = n_dev * SLOT
         dev_rows = ag[0].reshape(n_dev, SLOT, LANES)[:, 0:ONE, 0:SUB]
@@ -443,8 +456,8 @@
                            - scal[ww, rows, 0:w_] * left - scal[we, rows, 0:w_] * right)
                     v[rows, c0:c1] = out
                     parts = split3(out)
-                    for j in range(3):
-                        rp[j, rows, c0:c1] = parts[j]
+                    for j, part in enumerate(parts):
+                        rp[j, rows, c0:c1] = part
                     res = r[rows, c0:c1]
                     new = []
                     for total, t in zip(sums, (res * here, here * out, here * s[rows, c0:c1], res * res)):
@@ -596,12 +609,16 @@
             @pl.when(it > 0)
             def _():
                 field(par)
+                restrict(par)
                 pack_sides()
+                ag_start(par)
                 each(h_copy, 'start')
-                restrict(par)
-                ag_start(par)
 
             u[first_rows, :] = products(first_rows, 0, own)
+
+            @pl.when(it > 0)
+            def _():
+                ag_second(par)
             u[part_a, :] = products(part_a, 0, own)
             each(h_in, 'recv')
             for k in range(8):
@@ -627,7 +644,7 @@
 
             @pl.when(it > 0)
             def _():
-                ag_forward(par)
+                ag_third(par)
             u[part_b, :] = products(part_b, 0, k_main) + dot(lc[part_b, :], rc[...])
 
             @pl.when(it > 0)
@@ -656,7 +673,8 @@
         this, last = ITERS % TWO, (ITERS + ONE) % TWO
         field(this)
         ag_start(this)
-        ag_forward(this)
+        ag_second(this)
+        ag_third(this)
         forward(this).wait_recv()
         scalars(this, ITERS)
         advance()
@@ -670,7 +688,8 @@
             total = lax.fori_loop(0, size, line, jnp.zeros((SUB, c1 - c0), F32))
             ags[last, FOUR * h + 3:FOUR * h + FOUR, 0:c1 - c0] = rows_sum(total)
         ag_start(last)
-        ag_forward(last)
+        ag_second(last)
+        ag_third(last)
         forward(last).wait_recv()
         t = totals(last)
         for h, (c0, c1) in enumerate(halves):
@@ -717,13 +736,12 @@
         pltpu.VMEM((4, SUB, n_rhs), F32),
         pltpu.VMEM((ITERS + 2, 8, n_rhs), F32),
         pltpu.VMEM((5, own, 128), F32),
-        pltpu.VMEM((3 * kmax, own), F32),
         pltpu.SemaphoreType.DMA((edge // over,)),
         pltpu.SemaphoreType.DMA((2,)),
         pltpu.SemaphoreType.DMA((4,)), pltpu.SemaphoreType.DMA((4,)),
         pltpu.SemaphoreType.DMA((8,)), pltpu.SemaphoreType.DMA((8,)),
         pltpu.SemaphoreType.DMA((8,)), pltpu.SemaphoreType.DMA((8,)),
-    ] + [pltpu.SemaphoreType.DMA((TWO,))] * 4
+    ] + [pltpu.SemaphoreType.DMA((TWO,))] * 6
 
     return kernel, scratch
 

time: 209 us -> 239 us (1.14)
  Pallas kernels: 203 us -> 233 us
    pallas_call x1, Pallas kernels: 203 us -> 233 us  [body(): pl.pallas_call(kernel, out_shape=(jax.ShapeDtypeStruct((own, n_rhs), F32)...]
where the time goes in v2:
time: 239 us
  Pallas kernels  233 us (97%)
  local copies, waits for them, and re-layouts  4.2 us (2%)
    pallas_call x1, Pallas kernels, body(): pl.pallas_call(kernel, out_shape=(jax.ShapeDtypeStruct((own, n_rhs), F32)...  233 us

profile of v2, /device:TPU:97, one launch (start us, length us, event | category | flops | bytes accessed | tf_op | source)
XLA Modules:
  0.0 238.9 jit_solution(3980728242214429536)
XLA Ops:
  1.3 0.6 broadcast_in_dim.9.count_ref
  1.9 233.4 %shard_map.77 = (f32[1024,192]{1,0:T(8,128)}, f32[8,192]{1,0:T(8,128)}) custom-call(f32[1024,192]{1,0:T(8,128)} %bitcast.9, f32[32,32]{1,0:T(8,128)} %kappa_ref.1, f32[40,40,1600]{2,1,0:T(8,128)} %bitcast.7, f32[8,1024]{1,0:T(8,128)} %bitcast.10, f32[8,128]{1,0:T(8,128)} %broadcast_in_dim.9.count_ref, f32[128,128]{1,0:T(8,128)} %cinv_ref.1), custom_call_target="tpu_custom_call" | custom-call | tf_op jit(solution)/shard_map/pallas_call | solution.py:765
  235.3 2.3 copy.11
  237.6 1.3 copy.12

commit v3 on v2

--- a/solution.py
+++ b/solution.py
@@ -14,7 +14,10 @@
 OPP = (1, 0, 3, 2, 7, 6, 5, 4)
 COMBOS = ((0, 0), (0, 1), (1, 0), (0, 2), (1, 1), (2, 0))
 ONE, TWO, FOUR, SUB, LANES = 1, 2, 4, 8, 128
-SLOT = 3 * SUB
+SLOT = TWO * SUB
+RZ, ZW, RR = SUB, SUB + ONE, SUB + TWO
+TAIL_SUMS, TAIL_LAST = RR + ONE, RR + TWO
+PAIRS = ((SUB - ONE, 0, ONE), (TAIL_LAST, None, TWO), (TAIL_LAST + ONE, 3, FOUR), (TAIL_LAST + TWO, 5, 6))
 
 
 def repeat(count, body, by=ONE):
@@ -62,7 +65,6 @@
     h_len = [strip] * 4 + [corner] * 4
     halves = ((0, LANES), (LANES, n_rhs))
     tail = n_rhs - LANES
-    n_chip = n_dev // TWO
 
     def packed(rows):
         left = -(-rows // (TWO * SUB)) * SUB
@@ -79,12 +81,10 @@
                x_ref, norm_ref,
                nat, perm, stage, lp, lc, rp, rc, v, pack, h_out, halo, u, g_out, g_raw, g, r, p, s, ms, z, mc, ag, ags, cell_ref,
                coef, bcat, b_t, c_map, edges, pack_c, ring_v, cg, nb, scal,
-               l_sem, f_sem, e_send, e_recv, h_send, h_recv, g_send, g_recv, ag_send, ag_recv, up_send, up_recv, fw_send, fw_recv):
+               l_sem, f_sem, e_send, e_recv, h_send, h_recv, g_send, g_recv, ag_send, ag_recv):
         row_id = lax.axis_index('sx')
         col_id = lax.axis_index('sy')
         me = row_id * n_col + col_id
-        parity = row_id % TWO
-        my_slot = (row_id // TWO) * n_col + col_id
 
         def has(k):
             _, dr, dc = DIRS[k]
@@ -181,41 +181,19 @@
                     else:
                         copies[k].wait_send()
 
-        def own_slot(par):
-            return ag.at[par, 0, pl.ds(pl.multiple_of(my_slot * SLOT, SUB), SLOT)]
-
-        def ag_start(par):
-            ag[par, 0, pl.ds(pl.multiple_of(my_slot * SLOT, SUB), SLOT), :] = ags[par]
-            for d in range(ONE, n_col):
+        def ag_start(par, first=0):
+            rows = SLOT - first
+            mine = pl.ds(pl.multiple_of(me * SLOT + first, SUB), rows)
+            ag[par, mine, :] = ags[par, first:SLOT, :]
+            for d in range(ONE, n_dev):
+                peer = (me + d) % n_dev
                 pltpu.make_async_remote_copy(
-                    src_ref=ags.at[par], dst_ref=own_slot(par), send_sem=ag_send.at[par], recv_sem=ag_recv.at[par],
-                    device_id={'sy': (col_id + d) % n_col}, device_id_type=MESH).start()
-
-        def waits(par, sem, slots):
-            many = ag.at[par, 0, pl.ds(0, slots * SLOT)]
+                    src_ref=ags.at[par, pl.ds(first, rows)], dst_ref=ag.at[par, mine], send_sem=ag_send.at[par], recv_sem=ag_recv.at[par],
+                    device_id={'sx': peer // n_col, 'sy': peer % n_col}, device_id_type=MESH).start()
+
+        def ag_wait(par, sem, rows=SLOT):
+            many = ag.at[par, pl.ds(0, (n_dev - ONE) * rows)]
             pltpu.make_async_copy(many, many, sem.at[par]).wait()
-
-        def ag_second(par):
-            waits(par, ag_recv, n_col - ONE)
-            line = ag.at[par, 0, pl.ds(pl.multiple_of((row_id // TWO) * (n_col * SLOT), SUB), n_col * SLOT)]
-            for d in range(ONE, n_row // TWO):
-                pltpu.make_async_remote_copy(
-                    src_ref=line, dst_ref=line, send_sem=up_send.at[par], recv_sem=up_recv.at[par],
-                    device_id={'sx': (row_id + TWO * d) % n_row}, device_id_type=MESH).start()
-
-        def forward(par):
-            return pltpu.make_async_remote_copy(
-                src_ref=ag.at[par, 0], dst_ref=ag.at[par, ONE], send_sem=fw_send.at[par], recv_sem=fw_recv.at[par],
-                device_id={'sx': row_id + ONE - TWO * parity}, device_id_type=MESH)
-
-        def ag_third(par):
-            waits(par, up_recv, n_chip - n_col)
-            forward(par).start()
-
-        def ag_done(par):
-            waits(par, ag_send, n_col - ONE)
-            waits(par, up_send, n_chip - n_col)
-            forward(par).wait_send()
 
         def rows_sum(t):
             return jnp.sum(t, axis=0, keepdims=True)
@@ -255,11 +233,14 @@
             d2 = dot(b_t[0:16, :], rp[1, 0:own, :])
             d3 = dot(b_t[0:16, :], rp[2, 0:own, :])
             d = (d1[16:24] + d2[8:16] + d3[0:8]) + (d1[8:16] + d2[0:8]) + d1[0:8]
-            ags[par, SUB:TWO * SUB, :] = d[:, 0:LANES]
-            ags[par, TWO * SUB:SLOT, 0:tail] = d[:, LANES:n_rhs]
+            ags[par, 0:SUB - ONE, :] = d[0:SUB - ONE, 0:LANES]
+            for row, left, right in PAIRS:
+                if left is not None:
+                    ags[par, row:row + ONE, 0:tail] = d[left:left + ONE, LANES:n_rhs]
+                ags[par, row:row + ONE, tail:LANES] = d[right:right + ONE, LANES:n_rhs]
 
         restrict(0)
-        ags[0, 0:ONE, :] = count_ref[0:ONE, :]
+        ags[0, RZ:ZW, :] = count_ref[0:ONE, :]
         ag_start(0)
 
         for k in range(4):
@@ -267,8 +248,6 @@
             def _(k=k):
                 edge_in[k].wait_recv()
                 edge_copy[k].wait_send()
-
-        ag_second(0)
 
         def turn(count, col):
             for c0, c1 in tiles:
@@ -291,8 +270,6 @@
             for i in range(over):
                 stage[corner * q + over * i:corner * q + over * i + over, :] = nat[a0 + i, b0:b0 + over, :]
         turn(k_corner, k_main)
-
-        ag_third(0)
 
         def put_parts(rows, x, xc):
             parts = split3(x)
@@ -393,9 +370,9 @@
             scal[wd, rows, :] = a + b + c + d
         repeat(size, put_weights, FOUR)
 
-        forward(0).wait_recv()
+        ag_wait(0, ag_recv)
         n_slot = n_dev * SLOT
-        dev_rows = ag[0].reshape(n_dev, SLOT, LANES)[:, 0:ONE, 0:SUB]
+        dev_rows = ag[0].reshape(n_dev, SLOT, LANES)[:, RZ:ZW, 0:SUB]
         count_row = jnp.broadcast_to(dev_rows, (n_dev, SLOT, SUB)).reshape(n_slot, SUB).T
         count_dev = jnp.broadcast_to(dev_rows, (n_dev, SUB, SUB)).reshape(n_dev * SUB, SUB).T
 
@@ -406,12 +383,7 @@
             at = lax.broadcasted_iota(jnp.int32, shape, axis).astype(F32) * float(step)
             slot = floor_div(at, SLOT)
             inside = at - slot * SLOT
-            other = floor_div(slot, n_chip)
-            chip = slot - other * n_chip
-            line = floor_div(chip, n_col)
-            mine = parity.astype(F32)
-            odd = mine + other - TWO * mine * other
-            return (TWO * line + odd) * n_col + (chip - line * n_col), inside
+            return slot, inside
         sub_r, inside_r = slot_facts((n_dev * SUB, n_slot), 0, SLOT // SUB)
         sub_c, _ = slot_facts((n_dev * SUB, n_slot), ONE)
         before = jnp.where(jnp.logical_and(inside_r == 0.0, sub_r < sub_c), 1.0, 0.0).astype(F32)
@@ -419,11 +391,15 @@
         _, place = slot_facts((SUB, n_slot), ONE)
         which = lax.broadcasted_iota(jnp.int32, (ktot, n_slot), 0).astype(F32)
 
-        def one_hot(first):
-            here = place - first
+        def one_hot(here):
             target = jnp.where(jnp.logical_and(here >= 0.0, here < count_row), start_row + here, -1.0)
             return jnp.where(which == target[0:ONE, :], 1.0, 0.0).astype(F32)
-        pack_low, pack_high = one_hot(SUB), one_hot(TWO * SUB)
+        pack_low = one_hot(place)
+        at_left = at_right = jnp.full_like(place, -1.0)
+        for row, left, right in PAIRS:
+            if left is not None:
+                at_left = jnp.where(place == float(row), float(left), at_left)
+            at_right = jnp.where(place == float(row), float(right), at_right)
         k_row = lax.broadcasted_iota(jnp.int32, (k5, n_slot), 0).astype(F32)
         block = floor_div(k_row, kmax)
         sub_k, inside_k = slot_facts((k5, n_slot), ONE)
@@ -433,12 +409,24 @@
             shift = DIRS[k][1] * n_col + DIRS[k][2]
             wanted = wanted + jnp.where(block == k + ONE, float(shift), 0.0)
             present = jnp.logical_or(present, jnp.logical_and(block == k + ONE, exists[k]))
-        chosen = jnp.logical_and(sub_k == wanted, inside_k == SUB + k_row - block * kmax)
+        chosen = jnp.logical_and(sub_k == wanted, inside_k == k_row - block * kmax)
         select = jnp.where(jnp.logical_and(chosen, present), 1.0, 0.0).astype(F32)
         pick = lax.dot_general(select, pack_low, (((1,), (1,)), ((), ())), precision=lax.Precision.HIGHEST, preferred_element_type=F32)
         pick = dot_highest(pick, cinv_ref[...])
-        c_map[0:k5, :] = dot_highest(pick, pack_low)
-        c_map[k5:TWO * k5, :] = dot_highest(pick, pack_high)
+        for n, onto in enumerate((pack_low, one_hot(at_left), one_hot(at_right))):
+            c_map[k5 * n:k5 * n + k5, :] = dot_highest(pick, onto)
+
+        SUMS = (RZ, ZW, RR)
+
+        def place_of(h, row):
+            if not h:
+                return slice(row, row + ONE), slice(0, LANES)
+            at = TAIL_LAST if row == RR else TAIL_SUMS
+            return slice(at, at + ONE), (slice(tail, LANES) if row == ZW else slice(0, tail))
+
+        def put_sum(par, h, row, value):
+            rows, lanes = place_of(h, row)
+            ags[par, rows, lanes] = value
 
         def field(par):
             for h, (c0, c1) in enumerate(halves):
@@ -460,7 +448,7 @@
                         rp[j, rows, c0:c1] = part
                     res = r[rows, c0:c1]
                     new = []
-                    for total, t in zip(sums, (res * here, here * out, here * s[rows, c0:c1], res * res)):
+                    for total, t in zip(sums, (res * here, here * out, res * res)):
                         q = t[0:SUB]
                         for n in range(SUB, size, SUB):
                             q = q + t[n:n + SUB]
@@ -471,12 +459,17 @@
                     for n in range(FOUR):
                         sums = line(i * FOUR + n, sums)
                     return sums
-                sums = lax.fori_loop(0, size // FOUR, lines, tuple(jnp.zeros((SUB, w_), F32) for _ in range(FOUR)))
-                for n in range(FOUR):
-                    ags[par, FOUR * h + n:FOUR * h + n + ONE, 0:w_] = rows_sum(sums[n])
+                sums = lax.fori_loop(0, size // FOUR, lines, tuple(jnp.zeros((SUB, w_), F32) for _ in SUMS))
+                for n, total in zip(SUMS, sums):
+                    put_sum(par, h, n, rows_sum(total))
 
         def totals(par):
-            return jnp.sum(ag[par].reshape(n_dev, SLOT, LANES)[:, 0:SUB, :], axis=0)
+            t = jnp.sum(ag[par].reshape(n_dev, SLOT, LANES)[:, SUB:SLOT, :], axis=0)
+
+            def get(h, row):
+                rows, lanes = place_of(h, row)
+                return t[rows.start - SUB:rows.stop - SUB, lanes]
+            return get
 
         def products(rows, k0, k1):
             out = None
@@ -488,12 +481,12 @@
         def scalars(par, it):
             t = totals(par)
             for h, (c0, c1) in enumerate(halves):
-                rz, zw, zs, rr = [t[FOUR * h + n:FOUR * h + n + ONE, 0:c1 - c0] for n in range(FOUR)]
+                rz, zw, rr = [t(h, row) for row in SUMS]
                 nb[it, :, c0:c1] = jnp.broadcast_to(rr, (SUB, c1 - c0))
                 old_rz, old_pq = cg[0, 0:ONE, c0:c1], cg[ONE, 0:ONE, c0:c1]
                 first = it <= ONE
                 beta = jnp.where(first, 0.0, rz / old_rz)
-                pq = zw + jnp.where(first, 0.0, 2.0 * beta * zs + beta * beta * old_pq)
+                pq = zw - jnp.where(first, 0.0, beta * beta * old_pq)
                 for n, value in enumerate((rz, pq, rz / pq, beta)):
                     cg[n, 0:ONE, c0:c1] = value
 
@@ -609,16 +602,12 @@
             @pl.when(it > 0)
             def _():
                 field(par)
+                pack_sides()
+                each(h_copy, 'start')
                 restrict(par)
-                pack_sides()
                 ag_start(par)
-                each(h_copy, 'start')
 
             u[first_rows, :] = products(first_rows, 0, own)
-
-            @pl.when(it > 0)
-            def _():
-                ag_second(par)
             u[part_a, :] = products(part_a, 0, own)
             each(h_in, 'recv')
             for k in range(8):
@@ -641,15 +630,11 @@
                 pack_message(g_out, m_off[k], u, u_off[k], u_len[k])
             each(g_copy, 'start')
             u[part_a, :] = u[part_a, :] + (products(part_a, own, k_main) + dot(lc[part_a, :], rc[...]))
+            u[part_b, :] = products(part_b, 0, k_main) + dot(lc[part_b, :], rc[...])
 
             @pl.when(it > 0)
             def _():
-                ag_third(par)
-            u[part_b, :] = products(part_b, 0, k_main) + dot(lc[part_b, :], rc[...])
-
-            @pl.when(it > 0)
-            def _():
-                forward(par).wait_recv()
+                ag_wait(par, ag_recv)
                 scalars(par, it)
                 advance()
 
@@ -657,8 +642,8 @@
             def _():
                 cg[TWO, 0:ONE, :] = jnp.full((ONE, n_rhs), -1.0, F32)
 
-            c = dot_highest(c_map[...], ag[par].reshape(n_slot, LANES))
-            for (c0, c1), value in zip(halves, (c[0:k5], c[k5:TWO * k5, 0:tail])):
+            c = dot_highest(c_map[...], ag[par])
+            for (c0, c1), value in zip(halves, (c[0:k5], c[k5:TWO * k5, 0:tail] + c[TWO * k5:, tail:LANES])):
                 parts = split3(value)
                 for n, (_, j) in enumerate(COMBOS):
                     coef[k5 * n:k5 * n + k5, c0:c1] = parts[j].astype(F32)
@@ -667,15 +652,13 @@
             fold()
             each(h_copy, 'sent')
             each(g_copy, 'sent')
-            ag_done(par)
+            ag_wait(par, ag_send)
         repeat(ITERS, iteration)
 
         this, last = ITERS % TWO, (ITERS + ONE) % TWO
         field(this)
-        ag_start(this)
-        ag_second(this)
-        ag_third(this)
-        forward(this).wait_recv()
+        ag_start(this, SUB)
+        ag_wait(this, ag_recv, SUB)
         scalars(this, ITERS)
         advance()
         for h, (c0, c1) in enumerate(halves):
@@ -686,19 +669,17 @@
                     total = total + t[n:n + SUB]
                 return total
             total = lax.fori_loop(0, size, line, jnp.zeros((SUB, c1 - c0), F32))
-            ags[last, FOUR * h + 3:FOUR * h + FOUR, 0:c1 - c0] = rows_sum(total)
-        ag_start(last)
-        ag_second(last)
-        ag_third(last)
-        forward(last).wait_recv()
+            put_sum(last, h, RR, rows_sum(total))
+        ag_start(last, SUB)
+        ag_wait(last, ag_recv, SUB)
         t = totals(last)
         for h, (c0, c1) in enumerate(halves):
-            nb[ITERS + ONE, :, c0:c1] = jnp.broadcast_to(t[FOUR * h + 3:FOUR * h + FOUR, 0:c1 - c0], (SUB, c1 - c0))
+            nb[ITERS + ONE, :, c0:c1] = jnp.broadcast_to(t(h, RR), (SUB, c1 - c0))
         base_norm = jnp.sqrt(nb[ONE])
         for k in range(ITERS):
             norm_ref[k:k + ONE, :] = (jnp.sqrt(nb[k + TWO]) / base_norm)[0:ONE]
-        ag_done(this)
-        ag_done(last)
+        ag_wait(this, ag_send, SUB)
+        ag_wait(last, ag_send, SUB)
 
     COMBOS_C = ((0, 0), (0, 1), (0, 2), (1, 0), (1, 1), (2, 0))
     scratch = [
@@ -723,13 +704,13 @@
         pltpu.VMEM((size + 2, ring, n_rhs), F32),
         pltpu.VMEM((size + 2, ring, n_rhs), F32),
         pltpu.VMEM((own + 4 * size, n_rhs), F32),
-        pltpu.VMEM((TWO, TWO, n_chip * SLOT, LANES), F32),
+        pltpu.VMEM((TWO, n_dev * SLOT, LANES), F32),
         pltpu.VMEM((TWO, SLOT, LANES), F32),
         pltpu.VMEM((own, TWO * LANES), F32),
         pltpu.VMEM((256, n_rhs), F32),
         pltpu.VMEM((own + 4 * size, 256), BF16),
         pltpu.VMEM((3 * kmax, own), BF16),
-        pltpu.VMEM((10 * kmax, n_dev * SLOT), F32),
+        pltpu.VMEM((15 * kmax, n_dev * SLOT), F32),
         pltpu.VMEM((4, size, 256), F32),
         pltpu.VMEM((2, size, 256), F32),
         pltpu.VMEM((4, size, n_rhs), F32),
@@ -741,7 +722,7 @@
         pltpu.SemaphoreType.DMA((4,)), pltpu.SemaphoreType.DMA((4,)),
         pltpu.SemaphoreType.DMA((8,)), pltpu.SemaphoreType.DMA((8,)),
         pltpu.SemaphoreType.DMA((8,)), pltpu.SemaphoreType.DMA((8,)),
-    ] + [pltpu.SemaphoreType.DMA((TWO,))] * 6
+    ] + [pltpu.SemaphoreType.DMA((TWO,))] * 2
 
     return kernel, scratch
 

time: 239 us -> 192 us (0.80)
  Pallas kernels: 233 us -> 186 us
    pallas_call x1, Pallas kernels: 233 us -> 186 us  [body(): pl.pallas_call(kernel, out_shape=(jax.ShapeDtypeStruct((own, n_rhs), F32)...]
where the time goes in v3:
time: 192 us
  Pallas kernels  186 us (97%)
  local copies, waits for them, and re-layouts  4.2 us (2%)
    pallas_call x1, Pallas kernels, body(): pl.pallas_call(kernel, out_shape=(jax.ShapeDtypeStruct((own, n_rhs), F32)...  186 us

profile of v3, /device:TPU:97, one launch (start us, length us, event | category | flops | bytes accessed | tf_op | source)
XLA Modules:
  0.0 191.7 jit_solution(15875905318920542482)
XLA Ops:
  1.3 0.6 broadcast_in_dim.9.count_ref
  1.9 186.2 %shard_map.77 = (f32[1024,192]{1,0:T(8,128)}, f32[8,192]{1,0:T(8,128)}) custom-call(f32[1024,192]{1,0:T(8,128)} %bitcast.9, f32[32,32]{1,0:T(8,128)} %kappa_ref.1, f32[40,40,1600]{2,1,0:T(8,128)} %bitcast.7, f32[8,1024]{1,0:T(8,128)} %bitcast.10, f32[8,128]{1,0:T(8,128)} %broadcast_in_dim.9.count_ref, f32[128,128]{1,0:T(8,128)} %cinv_ref.1), custom_call_target="tpu_custom_call" | custom-call | tf_op jit(solution)/shard_map/pallas_call | solution.py:746
  188.1 2.3 %copy.11 = f32[32,32,192]{2,1,0:T(8,128)} copy(f32[32,32,192]{2,1,0:T(8,128)} %bitcast.8) | data formatting | bytes 1572864
  190.4 1.3 copy.12
